TPU v7x, 32 devices: a whole 2x2x4 slice. The times are simulated.
32 devices in a mesh: grp: 4 (over x, core), lat: 8 (over z, y).
Axes of the slice: x: 2, y: 2, z: 4, core: 2. Of those that a mesh axis runs over, the one named last changes fastest.
Arguments:
- grid_state: bfloat16 [16, 192, 384, 128], P('grp', 'lat'), may hold values from -6 to 6
- noise_field: bfloat16 [16, 192, 384, 128], P('grp', 'lat'), may hold values from -6 to 6
- legendre: bfloat16 [192, 128, 128], P('lat'), may hold values from -0.4375 to 0.4375
- diffusion: float32 [128], replicated, may hold values from 0.1 to 10
- input_weight: bfloat16 [128, 256], replicated, may hold values from -0.5 to 0.5
- noise_weight: bfloat16 [128, 256], replicated, may hold values from -0.5 to 0.5
- input_bias: float32 [256], replicated, may hold values from -4 to 4
- middle_weight: bfloat16 [256, 256], replicated, may hold values from -0.375 to 0.375
- output_weight: bfloat16 [256, 128], replicated, may hold values from -0.375 to 0.375
Outputs:
- new_state: bfloat16 [16, 192, 384, 128], P('grp', 'lat')
- ens_mean: float32 [192, 384, 128], P('lat')
- ens_var: float32 [192, 384, 128], P('lat')
All inputs are finite; a program needn't handle non-finite values.
Results may differ from a plain program's by a relative error of at most 0.012.
Values may be sent and summed in bfloat16 or wider, within the bound.
A program may use at most 192 MiB of HBM per device.

v0:
```python
import functools
import math

import jax
import jax.numpy as jnp
from jax import lax
from jax.experimental import pallas as pl
from jax.experimental.pallas import tpu as pltpu
from jax.sharding import PartitionSpec as P


BF16 = jnp.bfloat16
F32 = jnp.float32


def wave_table(lon_count, wave_count):
    lon_ids = jnp.arange(lon_count, dtype=jnp.int32)[:, None]
    wave_ids = jnp.arange(wave_count, dtype=jnp.int32)[None, :]
    phase = (lon_ids * wave_ids % lon_count).astype(jnp.float32) * (2.0 * math.pi / lon_count)
    factor = math.sqrt(2.0 / lon_count)
    joined = jnp.concatenate([jnp.cos(phase), -jnp.sin(phase)], axis=1) * factor
    return joined.astype(jnp.bfloat16)


def damping_filter(diffusion, wave_count):
    degree = jnp.arange(wave_count, dtype=jnp.int32).astype(jnp.float32)
    ratio = degree * (degree + 1.0) / float((wave_count - 1) * wave_count)
    return 1.0 / (1.0 + diffusion[None, :] * (ratio * ratio)[:, None])


def analysis_body(table_ref, grid_ref, out_ref):
    bands, _, rows, width, channels = out_ref.shape
    for row in range(0, rows, 2):
        pair = jnp.concatenate([grid_ref[0, row], grid_ref[0, row + 1]], axis=1)
        waves = jnp.dot(table_ref[...], pair, preferred_element_type=F32).astype(BF16)
        for k in range(2):
            out_ref[:, 0, row + k] = waves[:, k * channels:(k + 1) * channels].reshape(
                bands, width, channels
            )


def analyse(grid_state, table, first, count, bands):
    _, lat_rows, lon_count, channels = grid_state.shape
    width = table.shape[0] // bands
    rows = 6
    return pl.pallas_call(
        analysis_body,
        grid=(count, lat_rows // rows),
        in_specs=[
            pl.BlockSpec(table.shape, lambda b, i: (0, 0)),
            pl.BlockSpec((1, rows, lon_count, channels), lambda b, i: (b + first, i, 0, 0)),
        ],
        out_specs=pl.BlockSpec((bands, 1, rows, width, channels), lambda b, i: (0, b, i, 0, 0)),
        out_shape=jax.ShapeDtypeStruct((bands, count, lat_rows, width, channels), BF16),
        cost_estimate=pl.CostEstimate(
            flops=2 * count * lat_rows * lon_count * channels * table.shape[0],
            bytes_accessed=4 * count * lat_rows * lon_count * channels,
            transcendentals=0,
        ),
    )(table, grid_state)


def spectral_body(parts, in_ref, basis_ref, flipped_ref, damping_ref, *rest):
    outs, (fin, fout) = rest[:parts], rest[parts:]
    bands, _, lat_rows, width, channels = in_ref.shape
    waves = basis_ref.shape[0]
    lats = bands * lat_rows
    span = lat_rows * width
    for s in range(bands):
        fin[pl.ds(s * span, span), :] = in_ref[s, 0].astype(F32).reshape(span, channels)
    damping = jnp.concatenate([damping_ref[...]] * 2, axis=1)
    for m in range(waves):
        values = jnp.concatenate(
            [fin[pl.ds(r * waves + m, lats, stride=width), :] for r in range(2)], axis=1
        ).astype(BF16)
        spectrum = jnp.dot(flipped_ref[m], values, preferred_element_type=F32)
        filtered = (spectrum * damping).astype(BF16)
        grid = jnp.dot(basis_ref[m], filtered, preferred_element_type=F32)
        for r in range(2):
            fout[pl.ds(r * waves + m, lats, stride=width), :] = grid[
                :, r * channels:(r + 1) * channels
            ]
    part_rows = lat_rows // parts
    for q in range(parts):
        for s in range(bands):
            start = (s * lat_rows + q * part_rows) * width
            outs[q][s, 0] = (
                fout[pl.ds(start, part_rows * width), :]
                .reshape(part_rows, width, channels)
                .astype(BF16)
            )


def spectral(received, basis, flipped, damping, parts):
    bands, count, lat_rows, width, channels = received.shape
    part_rows = lat_rows // parts
    whole = lambda a: pl.BlockSpec(a.shape, lambda b: (0,) * a.ndim)
    return pl.pallas_call(
        functools.partial(spectral_body, parts),
        grid=(count,),
        in_specs=[
            pl.BlockSpec((bands, 1, lat_rows, width, channels), lambda b: (0, b, 0, 0, 0)),
            whole(basis),
            whole(flipped),
            whole(damping),
        ],
        out_specs=[
            pl.BlockSpec((bands, 1, part_rows, width, channels), lambda b: (0, b, 0, 0, 0))
        ] * parts,
        out_shape=[
            jax.ShapeDtypeStruct((bands, count, part_rows, width, channels), BF16)
        ] * parts,
        scratch_shapes=[pltpu.VMEM((bands * lat_rows * width, channels), F32)] * 2,
        cost_estimate=pl.CostEstimate(
            flops=8 * count * basis.size * channels,
            bytes_accessed=4 * received.size,
            transcendentals=0,
        ),
    )(received, basis, flipped, damping)


def silu(value):
    half = 0.5 * value
    return half + half * jnp.tanh(half)


def physics_body(groups, *refs):
    fields = refs[:groups]
    noise_ref, table_ref, first_ref, bias_ref, middle_ref, last_ref = refs[groups:groups + 6]
    state_ref, stats_ref = refs[-2:]
    members, _, lon_count, channels = noise_ref.shape
    states = []
    for ref in fields:
        count = ref.shape[1]
        waves = jnp.concatenate(
            [ref[:, k, 0].reshape(-1, channels) for k in range(count)], axis=1
        )
        smoothed = jnp.dot(table_ref[...], waves, preferred_element_type=F32)
        for k in range(count):
            flat = smoothed[:, k * channels:(k + 1) * channels]
            b = len(states)
            joined = jnp.concatenate([flat.astype(BF16), noise_ref[b, 0]], axis=1)
            pre = jnp.dot(joined, first_ref[...], preferred_element_type=F32)
            one = silu(pre + bias_ref[...]).astype(BF16)
            two = silu(jnp.dot(one, middle_ref[...], preferred_element_type=F32)).astype(BF16)
            tendency = jnp.dot(two, last_ref[...], preferred_element_type=F32)
            state = (flat + tendency).astype(BF16)
            state_ref[b, 0] = state
            states.append(state)
    values = [s.astype(F32) for s in states]
    total = functools.reduce(jnp.add, values)
    mean = total * (1.0 / members)
    spread = functools.reduce(jnp.add, [jnp.square(v - mean) for v in values])
    half = lon_count // 2
    for h in range(2):
        stats_ref[h, 0, 0] = total[h * half:(h + 1) * half].astype(BF16)
        stats_ref[h, 1, 0] = spread[h * half:(h + 1) * half].astype(BF16)


def physics(fields, noise, table, first, bias, middle, last, part, previous):
    bands, _, part_rows, width, channels = fields[0].shape
    members, lat_rows, lon_count, noise_channels = noise.shape
    whole = lambda a: pl.BlockSpec(a.shape, lambda i: (0,) * a.ndim)
    at = part * part_rows
    specs = [
        pl.BlockSpec((bands, f.shape[1], 1, width, channels), lambda i: (0, 0, i, 0, 0))
        for f in fields
    ]
    specs.append(
        pl.BlockSpec((members, 1, lon_count, noise_channels), lambda i: (0, i + at, 0, 0))
    )
    params = [table, first, bias, middle, last]
    specs += [whole(a) for a in params]
    operands = [*fields, noise, *params]
    aliases = {}
    if previous is not None:
        aliases = {len(operands): 0}
        operands.append(previous)
        specs.append(pl.BlockSpec(memory_space=pl.ANY))
    columns = members * part_rows * lon_count
    hidden = middle.shape[0]
    return pl.pallas_call(
        functools.partial(physics_body, len(fields)),
        grid=(part_rows,),
        in_specs=specs,
        out_specs=[
            pl.BlockSpec((members, 1, lon_count, channels), lambda i: (0, i + at, 0, 0)),
            pl.BlockSpec((2, 2, 1, lon_count // 2, channels), lambda i: (0, 0, i, 0, 0)),
        ],
        out_shape=[
            jax.ShapeDtypeStruct((members, lat_rows, lon_count, channels), BF16),
            jax.ShapeDtypeStruct((2, 2, part_rows, lon_count // 2, channels), BF16),
        ],
        input_output_aliases=aliases,
        cost_estimate=pl.CostEstimate(
            flops=2 * columns * (first.size + middle.size + last.size + 256 * channels),
            bytes_accessed=8 * columns * channels,
            transcendentals=2 * columns * hidden,
        ),
    )(*operands)


def swap(value, bit):
    groups = lax.axis_size("grp")
    return lax.ppermute(value, "grp", [(g, g ^ bit) for g in range(groups)])


def join(a, b, count):
    a, b = a.astype(F32), b.astype(F32)
    total = a[0] + b[0]
    spread = (a[1] + b[1]) + jnp.square(a[0] - b[0]) * (0.5 / count)
    return total, spread


def pair_moments(stats, members):
    core = lax.axis_index("grp") % 2
    own = lax.dynamic_index_in_dim(stats, core, 0, keepdims=False)
    other = lax.dynamic_index_in_dim(stats, 1 - core, 0, keepdims=False)
    return jnp.stack(join(own, swap(other, 1), members)).astype(BF16)


def ensemble_moments(held, members):
    groups = lax.axis_size("grp")
    core = lax.axis_index("grp") % 2
    bit, count = 2, 2 * members
    while bit < groups:
        held = jnp.stack(join(held.astype(BF16), swap(held.astype(BF16), bit), count))
        bit, count = 2 * bit, 2 * count
    scale = jnp.array([1.0 / count, 1.0 / (count - 1)], F32)
    held = (held * scale[:, None, None, None]).astype(BF16)
    partner = swap(held, 1)
    low = jnp.where(core == 0, held, partner)
    high = jnp.where(core == 0, partner, held)
    return low, high


def direct_plan(
    grid_state,
    noise_field,
    legendre,
    diffusion,
    input_weight,
    noise_weight,
    input_bias,
    middle_weight,
    output_weight,
):
    members, lat_rows, lon_count, _ = grid_state.shape
    wave_count = legendre.shape[1]
    bands = lax.axis_size("lat")
    local_waves = wave_count // bands
    chunk = 2
    parts = 2
    transform = wave_table(lon_count, wave_count)
    table = (
        transform.reshape(lon_count, 2, bands, local_waves)
        .transpose(0, 2, 1, 3)
        .reshape(lon_count, 2 * wave_count)
    )
    table_t = table.T
    exchange = lambda v: lax.all_to_all(v, "lat", split_axis=0, concat_axis=0, tiled=True)
    damping = damping_filter(diffusion, wave_count)

    sent = [
        analyse(grid_state, table_t, b, chunk, bands) for b in range(0, members, chunk)
    ]
    groups = lax.axis_size("grp")
    turned = legendre.transpose(1, 0, 2).reshape(bands, local_waves * lat_rows, wave_count)
    share = local_waves * lat_rows // groups
    own = lax.dynamic_slice_in_dim(turned, lax.axis_index("grp") * share, share, axis=1)
    basis = lax.all_gather(exchange(own), "grp", axis=1, tiled=True)
    basis = basis.reshape(bands, local_waves, lat_rows, wave_count).transpose(1, 0, 2, 3)
    basis = basis.reshape(local_waves, bands * lat_rows, wave_count)
    zonal_ids = lax.axis_index("lat") * local_waves + jnp.arange(local_waves, dtype=jnp.int32)
    total_ids = jnp.arange(wave_count, dtype=jnp.int32)
    triangle = total_ids[None, :] >= zonal_ids[:, None]
    basis = jnp.where(triangle[:, None], basis, jnp.zeros_like(basis))
    flipped = basis.transpose(0, 2, 1)
    received = [exchange(s) for s in sent]
    banded = [spectral(r, basis, flipped, damping, parts) for r in received]

    first = jnp.concatenate([input_weight, noise_weight], axis=0)
    new_state = None
    moments = []
    for q in range(parts):
        fields = [exchange(g[q]) for g in banded]
        if moments:
            fields, moments[-1] = lax.optimization_barrier((fields, moments[-1]))
        new_state, stats = physics(
            fields, noise_field, table, first, input_bias[None], middle_weight,
            output_weight, q, new_state,
        )
        moments.append(ensemble_moments(pair_moments(stats, members), members))
    joined = [jnp.concatenate([low, high], axis=2) for low, high in moments]
    ens_mean = jnp.concatenate([j[0] for j in joined], axis=0).astype(F32)
    ens_var = jnp.concatenate([j[1] for j in joined], axis=0).astype(F32)
    return (new_state, ens_mean, ens_var)


GROUP = 8


def slot_table(lon_count, wave_count, share, lane_y, lanes):
    offset = jnp.arange(lanes, dtype=jnp.int32)[:, None, None, None]
    p = jnp.arange(2, dtype=jnp.int32)[None, :, None, None]
    part = jnp.arange(2, dtype=jnp.int32)[None, None, :, None]
    unit = (lane_y - offset) % lanes * share + jnp.arange(share, dtype=jnp.int32)[None, None, None, :]
    wave = jnp.where(p == 0, unit, wave_count - unit)
    wave = jnp.where(unit == 0, jnp.where(part == 0, 0, wave_count // 2), wave)
    wave, unit, p, part = jnp.broadcast_arrays(wave, unit, p, part)
    quarter = jnp.where(unit == 0, p, part) * lon_count
    lon_ids = jnp.arange(lon_count, dtype=jnp.int32)
    turn = (4 * (wave.reshape(-1, 1) * lon_ids[None, :]) + quarter.reshape(-1, 1)) % (4 * lon_count)
    phase = turn.astype(F32) * (0.5 * math.pi / lon_count)
    return (jnp.cos(phase) * math.sqrt(2.0 / lon_count)).astype(BF16)


WAIT = pl.BlockSpec(memory_space=pl.ANY)
MESH = pl.DeviceIdType.MESH


def pipeline_body(lanes, far, cuts, grid_ref, noise_ref, table_t_ref, turned_ref, diffusion_ref, first_ref, bias_ref,
                  middle_ref, last_ref, state_ref, table_out, *rest):
    fields = rest[:lanes]
    (kept, sent, own, other, back, blocks_ref, basis, flipped, table_ref, damping, rows_in, noise_in,
     rows_out) = rest[lanes:lanes + 13]
    rest = rest[lanes + 13:]
    scratch = rest[:2 * lanes]
    (row_sem, noise_sem, out_sem, field_sem, table_sem, basis_send, basis_recv, kept_send, kept_recv, own_send, own_recv, back_send,
     back_recv) = rest[2 * lanes:]
    members, lat_rows, _, channels = grid_ref.shape
    blocks, share, depth = kept.shape[1:4]
    slots, per, totals, _ = own.shape
    ahead = slots // 2
    wave_count = turned_ref.shape[0]
    pieces = per // 2
    groups = lat_rows // GROUP
    rows = 2 * GROUP
    pitch = scratch[0].shape[0] // share
    chunks = members * cuts
    index, team = lax.axis_index("lat"), lax.axis_index("grp")
    place, lane = index // lanes, index % lanes
    half = place // far
    dist = (1 - half) * (far - 1 - place) + half * (place - far)
    hub_place = far - 1 + half
    opposite = (far - half) * lanes + lane
    core = team % 2
    partner = team + 1 - 2 * core
    hub, leaf = dist == 0, dist > 0
    start = lane * share
    ranges = [pl.ds(q * per, per) for q in range(cuts)]

    def remote(src, dst, send, recv, **target):
        return pltpu.make_async_remote_copy(
            src_ref=src, dst_ref=dst, send_sem=send, recv_sem=recv, device_id=target, device_id_type=MESH
        )

    def hub_lane(dy):
        return hub_place * lanes + (lane + lanes - dy) % lanes

    def source_lane(k):
        return (hub_place + (2 * half - 1) * (k // lanes)) * lanes + (lane + k % lanes) % lanes

    def span(q):
        return (0, pieces + 1) if q == 0 else (pieces * q + 1, pieces)

    def spot(q, j):
        return j // pieces, pieces * q + (q + cuts - 1) // cuts + j % pieces

    def basis_copy(q, dy):
        low, size = span(q)
        at = pl.multiple_of((dist * lanes + dy) * depth, depth)
        return remote(
            blocks_ref.at[dy, pl.ds(low, size)], basis.at[core, pl.ds(low, size), pl.ds(at, depth)],
            basis_send.at[q, dy], basis_recv.at[q, dist * lanes + dy], lat=hub_lane(dy),
        )

    def basis_own(q):
        low, size = span(q)
        return pltpu.make_async_copy(
            blocks_ref.at[0, pl.ds(low, size)], basis.at[core, pl.ds(low, size), pl.ds(0, depth)],
            basis_recv.at[q, 0],
        )

    def send_basis(q):
        for dy in range(1, lanes):
            basis_copy(q, dy).start()

        @pl.when(leaf)
        def _():
            basis_copy(q, 0).start()

        @pl.when(hub)
        def _():
            basis_own(q).start()

    def arrange(q):
        row = lax.broadcasted_iota(jnp.int32, (lat_rows, totals), 1)
        flip = lax.broadcasted_iota(jnp.int32, (totals, totals), 0)
        flip = flip + lax.broadcasted_iota(jnp.int32, (totals, totals), 1) == totals - 1
        flip = flip.astype(F32).astype(BF16)
        low, size = span(q)
        for dy in range(lanes):
            turn = (lane + lanes - dy) % lanes
            for e in range(size):
                unit = turn * share + q * per + core * pieces + e
                if e == pieces:
                    unit = turn * share + wave_count // 2 * (1 - (turn + lanes - 1) // lanes)
                near = turned_ref[unit].astype(F32)
                mirrored = jnp.dot(
                    turned_ref[(wave_count - unit) % wave_count], flip, preferred_element_type=F32
                )
                near = jnp.where(row >= unit, near, 0.0).reshape(groups, 1, GROUP, totals)
                mirrored = jnp.where(row < unit, mirrored, 0.0).reshape(groups, 1, GROUP, totals)
                both = jnp.concatenate([near, mirrored], axis=1).reshape(depth, totals)
                blocks_ref[dy, low + e] = both.astype(BF16)

    def basis_swap(q, low, size):
        part = basis.at[core, pl.ds(low, size)]
        return remote(part, part, basis_send.at[q, lanes], basis_recv.at[q, blocks], grp=partner)

    def basis_ready(q, low, size):
        pltpu.make_async_copy(
            blocks_ref.at[0, pl.ds(low, size)], basis.at[core, pl.ds(low, size), pl.ds(0, depth)],
            basis_recv.at[q, 0],
        ).wait()
        for k in range(1, blocks):
            part = basis.at[core, pl.ds(low, size), pl.ds(k * depth, depth)]
            remote(part, part, basis_send.at[q, 0], basis_recv.at[q, k], lat=opposite).wait_recv()
        basis_swap(q, low, size).start()
        basis_swap(q, low, size).wait_recv()
        for side in range(2):
            for e in range(size):
                flipped[side, low + e] = basis[side, low + e].T

    def lane_copy(b, q, dy):
        return remote(
            sent.at[b, dy - 1, ranges[q]], kept.at[b, dy, ranges[q]], kept_send.at[b, q, dy - 1],
            kept_recv.at[b, q, dy], lat=place * lanes + (lane + lanes - dy) % lanes,
        )

    def kept_copy(b, q, dy):
        k = dist * lanes + dy
        return remote(
            kept.at[b, dy, ranges[q]], kept.at[b, k, ranges[q]], kept_send.at[b, q, lanes - 1 + dy],
            kept_recv.at[b, q, k], lat=hub_lane(0),
        )

    def kept_arrival(b, q, k):
        part = kept.at[b, k, pl.ds(q * per, per)]
        return remote(part, part, kept_send.at[b, q, 0], kept_recv.at[b, q, k], lat=opposite)

    def own_copy(c):
        return remote(own.at[c % slots], other.at[c], own_send.at[c], own_recv.at[c], lat=opposite)

    def back_copy(b, q, k):
        units = pl.ds(q * per, per)
        return remote(
            kept.at[b, k, units], back.at[b, k % lanes, units], back_send.at[b, q, k - 1],
            back_recv.at[b, q, k % lanes], lat=source_lane(k),
        )

    def back_arrival(b, q, dy):
        part = back.at[b, dy, pl.ds(q * per, per)]
        return remote(part, part, back_send.at[b, q, 0], back_recv.at[b, q, dy], lat=opposite)

    def load(ref, n):
        at = pl.multiple_of(n % groups * GROUP, GROUP)
        held, sem = (rows_in, row_sem) if ref is grid_ref else (noise_in, noise_sem)
        return pltpu.make_async_copy(ref.at[n // groups, pl.ds(at, GROUP)], held.at[n % 2], sem.at[n % 2])

    def store(n):
        at = pl.multiple_of(n % groups * GROUP, GROUP)
        return pltpu.make_async_copy(
            rows_out.at[n % 2], state_ref.at[n // groups, pl.ds(at, GROUP)], out_sem.at[n % 2]
        )

    def analyse_group(n, carry):
        b = n // groups
        at = pl.multiple_of(n % groups * rows, rows)

        @pl.when(n + 1 < members * groups)
        def _():
            load(grid_ref, n + 1).start()

        load(grid_ref, n).wait()
        for k in range(0, GROUP, 2):
            pair = jnp.concatenate([rows_in[n % 2, k], rows_in[n % 2, k + 1]], axis=1)
            waves = jnp.dot(table_t_ref[...], pair, preferred_element_type=F32)
            row = 0
            for dy in range(lanes):
                for p in range(2):
                    for part in range(2):
                        for t in range(2):
                            scratch[2 * dy + part][pl.ds(p * GROUP + k + t, share, stride=pitch), :] = (
                                waves[row:row + share, t * channels:(t + 1) * channels]
                            )
                        row += share
        for dy in range(lanes):
            for part in range(2):
                value = scratch[2 * dy + part][...].reshape(share, pitch, channels)[:, :rows].astype(BF16)
                side = slice(part * channels, (part + 1) * channels)
                if dy == 0:
                    kept[b, 0, :, pl.ds(at, rows), side] = value
                else:
                    sent[b, dy - 1, :, pl.ds(at, rows), side] = value
        return carry

    def partial(c):
        b, q = c // cuts, c % cuts

        @pl.when(c == 0)
        def _():
            basis_ready(0, 0, pieces + 1)

        @pl.when((c > 0) & (c < cuts))
        def _():
            basis_ready(c, pieces * c + 1, pieces)

        for k in range(1, blocks):
            kept_arrival(b, q, k).wait_recv()

        @pl.when(c >= slots)
        def _():
            own_copy(c - slots).wait_send()

        def unit(j, carry):
            values = jnp.concatenate([kept[b, k, q * per + j] for k in range(blocks)], axis=0)
            side, e = spot(q, j)
            sums = jnp.dot(flipped[side, e], values, preferred_element_type=F32)
            own[c % slots, j] = sums.astype(BF16)
            return carry

        for j in range(per):
            unit(j, 0)

        @pl.when(q == 0)
        def _():
            values = jnp.concatenate([kept[b, k, 0, :, channels:] for k in range(blocks)], axis=0)
            sums = jnp.dot(flipped[0, pieces], values, preferred_element_type=F32)
            own[c % slots, 0, :, channels:] = sums.astype(BF16)

        own_copy(c).start()

    def synthesise(c):
        b, q = c // cuts, c % cuts
        own_copy(c).wait_recv()
        row = lax.broadcasted_iota(jnp.int32, (totals, channels), 0)

        def damped(j, mark, side):
            total = own[c % slots, j, :, side].astype(F32) + other[c, j, :, side].astype(F32)
            return (total * jnp.where(row < mark, damping[1], damping[0])).astype(BF16)

        def put(i, grid, side):
            back[b, 0, i, :, side] = grid[:depth]
            for k in range(1, blocks):
                kept[b, k, i, :, side] = grid[k * depth:(k + 1) * depth]

        def unit(j, carry):
            mark = start + q * per + j
            value = jnp.concatenate(
                [damped(j, mark, slice(r * channels, (r + 1) * channels)) for r in range(2)], axis=1
            )
            at, e = spot(q, j)
            grid = jnp.dot(basis[at, e], value, preferred_element_type=F32).astype(BF16)
            put(q * per + j, grid, slice(None))
            return carry

        for j in range(per):
            unit(j, 0)

        @pl.when(q == 0)
        def _():
            mark = jnp.where(start == 0, totals // 2, start)
            side = slice(channels, 2 * channels)
            grid = jnp.dot(basis[0, pieces], damped(0, mark, side), preferred_element_type=F32).astype(BF16)
            put(0, grid, side)

        for k in range(1, blocks):
            back_copy(b, q, k).start()

    def column_group(b, g):
        n = b * groups + g
        at = pl.multiple_of(g * rows, rows)

        @pl.when(n + 1 < (members - 1) * groups)
        def _():
            load(noise_ref, n + 1).start()

        @pl.when(g == 0)
        def _():
            for q in range(cuts):
                for dy in range(lanes):
                    if dy > 0:
                        back_arrival(b, q, dy).wait_recv()
                    else:
                        @pl.when(leaf)
                        def _():
                            back_arrival(b, q, dy).wait_recv()

        for dy in range(lanes):
            for part in range(2):
                side = slice(part * channels, (part + 1) * channels)
                value = back[b, dy, :, pl.ds(at, rows), side].astype(F32)
                space = jnp.zeros((share, pitch - rows, channels), F32)
                scratch[2 * dy + part][...] = jnp.concatenate([value, space], axis=1).reshape(-1, channels)
        load(noise_ref, n).wait()

        @pl.when(n >= 2)
        def _():
            store(n - 2).wait()

        def pair(i, carry):
            waves = []
            for t in range(2):
                waves.append(jnp.concatenate([
                    scratch[2 * dy + part][pl.ds(p * GROUP + 2 * i + t, share, stride=pitch), :]
                    for dy in range(lanes) for p in range(2) for part in range(2)
                ], axis=0).astype(BF16))
            smoothed = jnp.dot(table_ref[...], jnp.concatenate(waves, axis=1), preferred_element_type=F32)
            for t in range(2):
                flat = smoothed[:, t * channels:(t + 1) * channels]
                joined = jnp.concatenate([flat.astype(BF16), noise_in[n % 2, 2 * i + t]], axis=1)
                pre = jnp.dot(joined, first_ref[...], preferred_element_type=F32)
                one = silu(pre + bias_ref[...]).astype(BF16)
                two = silu(jnp.dot(one, middle_ref[...], preferred_element_type=F32)).astype(BF16)
                tendency = jnp.dot(two, last_ref[...], preferred_element_type=F32)
                rows_out[n % 2, 2 * i + t] = (flat + tendency).astype(BF16)
            return carry

        lax.fori_loop(0, GROUP // 2, pair, 0)
        store(n).start()

    def analyse_member(b, first):
        lax.fori_loop(b * groups, (b + 1) * groups, analyse_group, 0)
        for q in range(cuts):
            for dy in range(1, lanes):
                lane_copy(b, q, dy).start()
            if first and q == 0:
                for later in range(1, cuts):
                    arrange(later)
            if first and q + 1 < cuts:
                @pl.when(hub)
                def _():
                    send_basis(q + 1)

        @pl.when(leaf)
        def _():
            kept_copy(b, 0, 0).start()
            for q in range(cuts):
                for dy in range(1, lanes):
                    kept_arrival(b, q, dy).wait_recv()
                    kept_copy(b, q, dy).start()
                if q + 1 < cuts:
                    if first:
                        send_basis(q + 1)
                    kept_copy(b, q + 1, 0).start()

    load(grid_ref, 0).start()
    load(noise_ref, 0).start()
    arrange(0)
    send_basis(0)
    analyse_member(0, True)
    table_ref[...] = table_t_ref[...].T
    degree = lax.broadcasted_iota(jnp.int32, (totals, channels), 0)
    for side in range(2):
        n = (degree if side == 0 else totals - 1 - degree).astype(F32)
        ratio = n * (n + 1.0) / float((totals - 1) * totals)
        damping[side] = 1.0 / (1.0 + diffusion_ref[...] * (ratio * ratio))
    table_copy = pltpu.make_async_copy(table_ref, table_out, table_sem)
    table_copy.start()

    def tick(t, carry):
        @pl.when(hub)
        def _():
            @pl.when(t < chunks)
            def _():
                partial(t)

            @pl.when(t >= ahead)
            def _():
                synthesise(t - ahead)

        soon = t // cuts + 1

        @pl.when((t % cuts == 1) & (soon < members))
        def _():
            analyse_member(soon, False)

        late = t - cuts - ahead - 1
        g = (late + 2 * cuts) % cuts

        @pl.when((late >= 0) & (g < groups))
        def _():
            column_group(late // cuts, g)

        return carry

    lax.fori_loop(0, chunks + ahead, tick, 0)

    last = members - 1
    for q in range(cuts):
        for dy in range(lanes):
            if dy > 0:
                back_arrival(last, q, dy).wait_recv()
            else:
                @pl.when(leaf)
                def _():
                    back_arrival(last, q, dy).wait_recv()
    finals = [
        pltpu.make_async_copy(back.at[last, dy], fields[dy].at[0], field_sem.at[dy]) for dy in range(lanes)
    ]
    for dy in range(1, lanes):
        finals[dy].start()
    finals[0].start()
    for n in ((members - 1) * groups - 2, (members - 1) * groups - 1):
        store(n).wait()

    def drain(b, carry):
        for q in range(cuts):
            for dy in range(1, lanes):
                lane_copy(b, q, dy).wait_send()

            @pl.when(leaf)
            def _():
                for dy in range(lanes):
                    kept_copy(b, q, dy).wait_send()

            @pl.when(hub)
            def _():
                for k in range(1, blocks):
                    back_copy(b, q, k).wait_send()
        return carry

    lax.fori_loop(0, members, drain, 0)

    @pl.when(hub)
    def _():
        for q in range(cuts):
            basis_swap(q, *span(q)).wait_send()
        for c in range(chunks - slots, chunks):
            own_copy(c).wait_send()

    @pl.when(leaf)
    def _():
        for q in range(cuts):
            basis_copy(q, 0).wait_send()

    for q in range(cuts):
        for dy in range(1, lanes):
            basis_copy(q, dy).wait_send()
    table_copy.wait()
    for final in finals:
        final.wait()


def pipeline(lanes, far, cuts, grid_state, noise, table_t, turned, diffusion, first, bias, middle, output):
    members, lat_rows, lon_count, channels = grid_state.shape
    wave_count = turned.shape[0]
    share = wave_count // 2 // lanes
    entries = share // 2 + 1
    depth = 2 * lat_rows
    count = far * lanes
    per = share // cuts
    slots = 6
    vmem = pl.BlockSpec(memory_space=pltpu.VMEM)
    dma = pltpu.SemaphoreType.DMA
    return pl.pallas_call(
        functools.partial(pipeline_body, lanes, far, cuts),
        in_specs=[WAIT, WAIT, vmem, vmem, vmem, vmem, vmem, vmem, vmem],
        out_specs=[WAIT] * (2 + lanes),
        out_shape=[
            jax.ShapeDtypeStruct((members - 1, *grid_state.shape[1:]), BF16),
            jax.ShapeDtypeStruct((lon_count, table_t.shape[0]), BF16),
        ] + [jax.ShapeDtypeStruct((1, share, depth, 2 * channels), BF16)] * lanes,
        scratch_shapes=[
            pltpu.VMEM((members, count, share, depth, 2 * channels), BF16),
            pltpu.VMEM((members, lanes - 1, share, depth, 2 * channels), BF16),
            pltpu.VMEM((slots, per, wave_count, 2 * channels), BF16),
            pltpu.VMEM((members * cuts, per, wave_count, 2 * channels), BF16),
            pltpu.VMEM((members, lanes, share, depth, 2 * channels), BF16),
            pltpu.VMEM((lanes, entries, depth, wave_count), BF16),
            pltpu.VMEM((2, entries, count * depth, wave_count), BF16),
            pltpu.VMEM((2, entries, wave_count, count * depth), BF16),
            pltpu.VMEM((lon_count, table_t.shape[0]), BF16),
            pltpu.VMEM((2, wave_count, channels), F32),
        ] + [pltpu.VMEM((2, GROUP, lon_count, channels), BF16)] * 3 + [pltpu.VMEM((share * 3 * GROUP, channels), F32)] * (2 * lanes) + [
            dma((2,)),
            dma((2,)),
            dma((2,)),
            dma((lanes,)),
            dma,
            dma((cuts, lanes + 1)),
            dma((cuts, count + 1)),
            dma((members, cuts, 2 * lanes - 1)),
            dma((members, cuts, count)),
            dma((members * cuts,)),
            dma((members * cuts,)),
            dma((members, cuts, count - 1)),
            dma((members, cuts, lanes)),
        ],
        compiler_params=pltpu.CompilerParams(
            has_side_effects=True, vmem_limit_bytes=64000 * 1024
        ),
    )(grid_state, noise, table_t, turned, diffusion, first, bias, middle, output)


def last_body(lanes, *refs):
    core_ref, fields = refs[0], refs[1:1 + lanes]
    noise_ref, table_ref, first_ref, bias_ref, middle_ref, last_ref, held_ref = refs[1 + lanes:8 + lanes]
    state_ref, mine_ref, give_ref = refs[-2 * lanes - 3:-2 * lanes]
    scratch = refs[-2 * lanes:]
    members, lats, lon_count, channels = state_ref.shape
    _, share, rows, _ = fields[0].shape
    pitch = scratch[0].shape[0] // share
    inner = pl.program_id(0)

    @pl.when(inner == 0)
    def _():
        for dy in range(lanes):
            for part in range(2):
                value = fields[dy][0, :, :, part * channels:(part + 1) * channels].astype(F32)
                space = jnp.zeros((share, pitch - rows, channels), F32)
                scratch[2 * dy + part][...] = jnp.concatenate([value, space], axis=1).reshape(-1, channels)

    waves = []
    for k in range(lats):
        at = inner * lats + k
        waves.append(jnp.concatenate([
            scratch[2 * dy + part][pl.ds(p * rows // 2 + at, share, stride=pitch), :]
            for dy in range(lanes) for p in range(2) for part in range(2)
        ], axis=0).astype(BF16))
    smoothed = jnp.dot(table_ref[...], jnp.concatenate(waves, axis=1), preferred_element_type=F32)
    half = lon_count // 2
    for k in range(lats):
        flat = smoothed[:, k * channels:(k + 1) * channels]
        joined = jnp.concatenate([flat.astype(BF16), noise_ref[0, k]], axis=1)
        pre = jnp.dot(joined, first_ref[...], preferred_element_type=F32)
        one = silu(pre + bias_ref[...]).astype(BF16)
        two = silu(jnp.dot(one, middle_ref[...], preferred_element_type=F32)).astype(BF16)
        tendency = jnp.dot(two, last_ref[...], preferred_element_type=F32)
        state = (flat + tendency).astype(BF16)
        for b in range(members - 1):
            state_ref[b, k] = held_ref[b, k]
        state_ref[members - 1, k] = state
        values = [held_ref[b, k].astype(F32) for b in range(members - 1)] + [state.astype(F32)]
        total = functools.reduce(jnp.add, values)
        mean = total * (1.0 / members)
        spread = functools.reduce(jnp.add, [jnp.square(v - mean) for v in values])
        sums = [total.astype(BF16), spread.astype(BF16)]
        for h in range(2):
            @pl.when(core_ref[0] == h)
            def _():
                for j in range(2):
                    mine_ref[j, k] = sums[j][h * half:(h + 1) * half]
                    give_ref[j, k] = sums[j][(1 - h) * half:(2 - h) * half]


def last_columns(fields, core, noise, table, first, bias, middle, output, states, part, previous, after):
    lanes = len(fields)
    members, _, lon_count, channels = noise.shape
    _, share, _, width = fields[0].shape
    rows = 2 * GROUP
    lats = 2
    inner = GROUP // lats
    half = lon_count // 2
    whole = lambda a: pl.BlockSpec(a.shape, lambda i: (0,) * a.ndim)
    params = [table, first, bias, middle, output]
    operands = [core, *fields, noise, *params, states]
    specs = [pl.BlockSpec(memory_space=pltpu.SMEM)]
    specs += [pl.BlockSpec((1, share, rows, width), lambda i: (0, 0, part, 0))] * lanes
    specs.append(pl.BlockSpec(
        (1, lats, lon_count, channels), lambda i: (members - 1, part * inner + i, 0, 0)
    ))
    specs += [whole(a) for a in params]
    specs.append(pl.BlockSpec(
        (members - 1, lats, lon_count, channels), lambda i: (0, part * inner + i, 0, 0)
    ))
    aliases = {}
    if previous is not None:
        aliases = {len(operands): 0}
        operands.append(previous)
    operands += after
    specs += [WAIT] * (len(operands) - len(specs))
    points = GROUP * lon_count
    hidden = middle.shape[0]
    return pl.pallas_call(
        functools.partial(last_body, lanes),
        grid=(inner,),
        in_specs=specs,
        out_specs=[
            pl.BlockSpec((members, lats, lon_count, channels), lambda i: (0, part * inner + i, 0, 0))
        ] + [pl.BlockSpec((2, lats, half, channels), lambda i: (0, i, 0, 0))] * 2,
        out_shape=[
            jax.ShapeDtypeStruct(noise.shape, BF16)
        ] + [jax.ShapeDtypeStruct((2, GROUP, half, channels), BF16)] * 2,
        input_output_aliases=aliases,
        scratch_shapes=[pltpu.VMEM((share * 3 * GROUP, channels), F32)] * (2 * lanes),
        cost_estimate=pl.CostEstimate(
            flops=2 * points * (first.size + middle.size + output.size + 256 * channels),
            bytes_accessed=16 * points * channels,
            transcendentals=2 * points * hidden,
        ),
    )(*operands)


def blend_body(count, scales, one_ref, two_ref, out_ref):
    total, spread = join(one_ref[...], two_ref[...], count)
    out_ref[0] = (total * scales[0]).astype(BF16)
    out_ref[1] = (spread * scales[1]).astype(BF16)


def blend(one, two, count, scales):
    _, group, half, channels = one.shape
    block = pl.BlockSpec((2, 4, half, channels), lambda i: (0, i, 0, 0))
    return pl.pallas_call(
        functools.partial(blend_body, count, scales),
        grid=(group // 4,),
        in_specs=[block, block],
        out_specs=block,
        out_shape=jax.ShapeDtypeStruct(one.shape, BF16),
        cost_estimate=pl.CostEstimate(
            flops=4 * one.size, bytes_accessed=6 * one.size, transcendentals=0
        ),
    )(one, two)


def place_body(core_ref, mine_ref, partner_ref, *refs):
    outs = refs[-2:]
    half = mine_ref.shape[2]
    for h in range(2):
        @pl.when(core_ref[0] == h)
        def _():
            for j in range(2):
                outs[j][:, h * half:(h + 1) * half] = mine_ref[j].astype(F32)
                outs[j][:, (1 - h) * half:(2 - h) * half] = partner_ref[j].astype(F32)


def place_moments(core, mine, partner, part, lat_rows, previous):
    _, group, half, channels = mine.shape
    shape = (lat_rows, 2 * half, channels)
    block = pl.BlockSpec((2, 4, half, channels), lambda i: (0, i, 0, 0))
    return pl.pallas_call(
        place_body,
        grid=(group // 4,),
        in_specs=[pl.BlockSpec(memory_space=pltpu.SMEM), block, block] + [WAIT] * len(previous),
        out_specs=[
            pl.BlockSpec((4, 2 * half, channels), lambda i: (part * (group // 4) + i, 0, 0))
        ] * 2,
        out_shape=[jax.ShapeDtypeStruct(shape, F32)] * 2,
        input_output_aliases={3 + j: j for j in range(len(previous))},
        cost_estimate=pl.CostEstimate(
            flops=4 * mine.size, bytes_accessed=16 * mine.size, transcendentals=0
        ),
    )(core, mine, partner, *previous)


def hub_plan(
    lanes,
    grid_state,
    noise_field,
    legendre,
    diffusion,
    input_weight,
    noise_weight,
    input_bias,
    middle_weight,
    output_weight,
):
    members, lat_rows, lon_count, _ = grid_state.shape
    wave_count = legendre.shape[1]
    far = lax.axis_size("lat") // lanes // 2
    share = wave_count // 2 // lanes
    parts = lat_rows // GROUP
    cuts = 8
    lane = lax.axis_index("lat") % lanes
    core = lax.axis_index("grp") % 2
    table_t = slot_table(lon_count, wave_count, share, lane, lanes)
    first = jnp.concatenate([input_weight, noise_weight], axis=0)
    params = (first, input_bias[None], middle_weight, output_weight)
    turned = legendre.transpose(1, 0, 2)
    states, table, *fields = pipeline(
        lanes, far, cuts, grid_state, noise_field, table_t, turned, diffusion[None], *params
    )
    groups = lax.axis_size("grp")
    flag = core[None].astype(jnp.int32)
    new_state, after, placed = None, [], []
    for q in range(parts):
        new_state, mine, give = last_columns(
            fields, flag, noise_field, table, *params, states, q, new_state, after
        )
        held = blend(mine, swap(give, 1), members, (1.0, 1.0))
        after = [held]
        bit, count = 2, 2 * members
        while bit < groups:
            other = swap(held, bit)
            final = 2 * bit >= groups
            scales = (0.5 / count, 1.0 / (2 * count - 1)) if final else (1.0, 1.0)
            held = blend(held, other, count, scales)
            bit, count = 2 * bit, 2 * count
        partner = swap(held, 1)
        placed = place_moments(flag, held, partner, q, lat_rows, placed)
    return (new_state, *placed)


def lane_count(mesh):
    line = [getattr(d, "coords", None) for d in mesh.devices.reshape(-1, mesh.shape["lat"])[0]]
    if len(line) < 2 or line[0] is None:
        return 2
    axis = [a != b for a, b in zip(line[0], line[1])].index(True)
    return len({c[axis] for c in line})


def per_device(lanes, *args):
    grid_state, legendre = args[0], args[2]
    members, lat_rows = grid_state.shape[:2]
    units = legendre.shape[1] // 2
    fits = (
        lax.axis_size("lat") % (2 * lanes) == 0
        and units % (16 * lanes) == 0
        and lat_rows % GROUP == 0
        and lat_rows // GROUP < 7
        and members > 1
        and lax.axis_size("grp") > 2
    )
    return hub_plan(lanes, *args) if fits else direct_plan(*args)


def solution(mesh):
    in_specs = (
        P("grp", "lat", None, None),
        P("grp", "lat", None, None),
        P("lat", None, None),
        P(),
        P(),
        P(),
        P(),
        P(),
        P(),
    )
    out_specs = (P("grp", "lat", None, None), P("lat", None, None), P("lat", None, None))

    def body(*args):
        return per_device(lane_count(mesh), *args)

    return jax.shard_map(
        body, mesh=mesh, in_specs=in_specs, out_specs=out_specs, check_vma=False
    )
```

profile of v0, /device:TPU:0, one launch (start us, length us, event | category | flops | bytes accessed | tf_op | source)
XLA Modules:
  0.0 326.9 jit_solution(8662780286475668861)
XLA Ops:
  1.2 0.8 constant_dynamic-update-slice_fusion.1
  2.0 2.5 copy.20
  4.5 0.8 constant_dynamic-update-slice_fusion.first_ref.refs_5_
  5.4 2.5 fusion.4.table_t_ref
  7.8 215.1 %shard_map.112 = (bf16[3,24,384,128]{3,2,1,0:T(8,128)(2,1)}, bf16[384,256]{1,0:T(8,128)(2,1)}, bf16[1,32,48,256]{3,2,1,0:T(8,128)(2,1)}, bf16[1,32,48,256]{3,2,1,0:T(8,128)(2,1)}) custom-call(bf16[4,24,384,128]{3,2,1,0:T(8,128)(2,1)} %grid_ref.1, bf16[4,24,384,128]{3,2,1,0:T(8,128)(2,1)} %refs_3_.5, bf16[256,384]{1,0:T(8,128)(2,1)} %fusion.4.table_t_ref, ...), custom_call_target="tpu_custom_call" | custom-call | tf_op jit(solution)/shard_map/pallas_call | solution.py:768
  223.0 8.1 %shard_map.113 = (bf16[4,24,384,128]{3,2,1,0:T(8,128)(2,1)}, bf16[2,8,192,128]{3,2,1,0:T(8,128)(2,1)}, bf16[2,8,192,128]{3,2,1,0:T(8,128)(2,1)}) custom-call(s32[1]{0:T(128)} %bitcast.refs_0_.core_ref, bf16[1,32,48,256]{3,2,1,0:T(8,128)(2,1)} %get-tuple-element.22.refs_1_, bf16[1,32,48,256]{3,2,1,0:T(8,128)(2,1)} %get-tuple-element.23.refs_2_, ...), custom_call_target="tpu_custom_call" | custom-call | flops 1207959552 | bytes 6291456 | tf_op jit(solution)/shard_map/pallas_call | solution.py:887
  231.1 2.5 collective-permute-done.two_ref
  233.6 0.9 copy-done.7
  234.4 2.3 shard_map.114.refs_11_.one_ref
  236.7 8.1 %shard_map.115 = (bf16[4,24,384,128]{3,2,1,0:T(8,128)(2,1)}, bf16[2,8,192,128]{3,2,1,0:T(8,128)(2,1)}, bf16[2,8,192,128]{3,2,1,0:T(8,128)(2,1)}) custom-call(s32[1]{0:T(128)} %bitcast.refs_0_.core_ref, bf16[1,32,48,256]{3,2,1,0:T(8,128)(2,1)} %get-tuple-element.22.refs_1_, ...), custom_call_target="tpu_custom_call", output_to_operand_aliasing={{0}: (10, {})} | custom-call | flops 1207959552 | bytes 6291456 | tf_op jit(solution)/shard_map/pallas_call | solution.py:887
  245.0 2.4 collective-permute-done.1.two_ref
  247.3 0.9 copy-done.8
  248.2 2.3 shard_map.116.refs_11_.one_ref
  250.5 8.2 %shard_map.117 = (bf16[4,24,384,128]{3,2,1,0:T(8,128)(2,1)}, bf16[2,8,192,128]{3,2,1,0:T(8,128)(2,1)}, bf16[2,8,192,128]{3,2,1,0:T(8,128)(2,1)}) custom-call(s32[1]{0:T(128)} %bitcast.refs_0_.core_ref, bf16[1,32,48,256]{3,2,1,0:T(8,128)(2,1)} %get-tuple-element.22.refs_1_, ...), custom_call_target="tpu_custom_call", output_to_operand_aliasing={{0}: (10, {})} | custom-call | flops 1207959552 | bytes 6291456 | tf_op jit(solution)/shard_map/pallas_call | solution.py:887
  258.8 1.5 collective-permute-start.7
  261.2 0.9 copy-done.6
  262.1 2.3 shard_map.118.one_ref
  264.3 1.5 collective-permute-start.3
  265.8 13.5 %collective-permute-done.7.two_ref = bf16[2,8,192,128]{3,2,1,0:T(8,128)(2,1)} collective-permute-done((bf16[2,8,192,128]{3,2,1,0:T(8,128)(2,1)S(1)}, bf16[2,8,192,128]{3,2,1,0:T(8,128)(2,1)}, u32[]{:S(2)}, u32[]{:S(2)}) %collective-permute-start.7) | collective-permute-done | bytes 786464 | tf_op jit(solution)/shard_map/ppermute | solution.py:205
  279.3 2.3 shard_map.121.mine_ref
  281.7 14.4 %collective-permute-done.5.two_ref = bf16[2,8,192,128]{3,2,1,0:T(8,128)(2,1)S(1)} collective-permute-done((bf16[2,8,192,128]{3,2,1,0:T(8,128)(2,1)S(1)}, bf16[2,8,192,128]{3,2,1,0:T(8,128)(2,1)S(1)}, u32[]{:S(2)}, u32[]{:S(2)}) %collective-permute-start.5) | collective-permute-done | bytes 786464 | tf_op jit(solution)/shard_map/ppermute | solution.py:205
  296.1 0.9 copy-done.4
  297.0 2.3 shard_map.120.mine_ref
  299.3 13.1 %collective-permute-done.3.two_ref = bf16[2,8,192,128]{3,2,1,0:T(8,128)(2,1)S(1)} collective-permute-done((bf16[2,8,192,128]{3,2,1,0:T(8,128)(2,1)}, bf16[2,8,192,128]{3,2,1,0:T(8,128)(2,1)S(1)}, u32[]{:S(2)}, u32[]{:S(2)}) %collective-permute-start.3) | collective-permute-done | bytes 786464 | tf_op jit(solution)/shard_map/ppermute | solution.py:205
  312.3 0.9 copy-done.5
  313.2 2.3 shard_map.119.mine_ref
  315.5 0.9 copy-done.3
  316.4 2.9 shard_map.122
  319.3 0.9 copy-done.10
  320.2 2.9 shard_map.123
  323.1 0.9 copy-done.9
  324.0 2.9 shard_map.124
  (34 shorter events, 1.7 us)
Async XLA Ops:
  5.4 2.5 copy-start.2
  231.1 2.5 collective-permute-start
  233.6 0.9 copy-start.7
  244.8 2.5 collective-permute-start.1
  247.3 0.9 copy-start.8
  250.5 8.3 %copy-start = (bf16[2,8,192,128]{3,2,1,0:T(8,128)(2,1)S(1)}, bf16[2,8,192,128]{3,2,1,0:T(8,128)(2,1)}, u32[]{:S(2)}) copy-start(bf16[2,8,192,128]{3,2,1,0:T(8,128)(2,1)} %shard_map.114.refs_11_.one_ref) | copy-start | bytes 2359300
  250.5 9.8 %copy-start.1 = (bf16[2,8,192,128]{3,2,1,0:T(8,128)(2,1)S(1)}, bf16[2,8,192,128]{3,2,1,0:T(8,128)(2,1)}, u32[]{:S(2)}) copy-start(bf16[2,8,192,128]{3,2,1,0:T(8,128)(2,1)} %shard_map.116.refs_11_.one_ref) | copy-start | bytes 2359300
  258.7 2.5 collective-permute-start.2
  258.8 20.5 %collective-permute-start.7 = (bf16[2,8,192,128]{3,2,1,0:T(8,128)(2,1)S(1)}, bf16[2,8,192,128]{3,2,1,0:T(8,128)(2,1)}, u32[]{:S(2)}, u32[]{:S(2)}) collective-permute-start(bf16[2,8,192,128]{3,2,1,0:T(8,128)(2,1)S(1)} %copy-done), channel_id=1, source_target_pairs={{0,16},{8,24},{16,0},{24,8},{1,17},{9,25},{17,1},{25,9},{2,18},{10... | collective-permute-start | bytes 2359304 | tf_op jit(solution)/shard_map/ppermute | solution.py:205
  260.3 35.8 %collective-permute-start.5 = (bf16[2,8,192,128]{3,2,1,0:T(8,128)(2,1)S(1)}, bf16[2,8,192,128]{3,2,1,0:T(8,128)(2,1)S(1)}, u32[]{:S(2)}, u32[]{:S(2)}) collective-permute-start(bf16[2,8,192,128]{3,2,1,0:T(8,128)(2,1)S(1)} %copy-done.1), channel_id=1, source_target_pairs={{0,16},{8,24},{16,0},{24,8},{1,17},{9,25},{17,1},{25,9},{2,18},{10... | collective-permute-start | bytes 2359304 | tf_op jit(solution)/shard_map/ppermute | solution.py:205
  261.2 0.9 copy-start.6
  264.3 48.0 %collective-permute-start.3 = (bf16[2,8,192,128]{3,2,1,0:T(8,128)(2,1)}, bf16[2,8,192,128]{3,2,1,0:T(8,128)(2,1)S(1)}, u32[]{:S(2)}, u32[]{:S(2)}) collective-permute-start(bf16[2,8,192,128]{3,2,1,0:T(8,128)(2,1)} %shard_map.118.one_ref), channel_id=1, source_target_pairs={{0,16},{8,24},{16,0},{24,8},{1,17},{9,25},{17,1},{25,9},{2,18},{10... | collective-permute-start | bytes 2359304 | tf_op jit(solution)/shard_map/ppermute | solution.py:205
  281.7 33.9 %collective-permute-start.8 = (bf16[2,8,192,128]{3,2,1,0:T(8,128)(2,1)}, bf16[2,8,192,128]{3,2,1,0:T(8,128)(2,1)S(1)}, u32[]{:S(2)}, u32[]{:S(2)}) collective-permute-start(bf16[2,8,192,128]{3,2,1,0:T(8,128)(2,1)} %shard_map.121.mine_ref), channel_id=1, source_target_pairs={{0,8},{8,0},{16,24},{24,16},{1,9},{9,1},{17,25},{25,17},{2,10},{10... | collective-permute-start | bytes 2359304 | tf_op jit(solution)/shard_map/ppermute | solution.py:205
  296.1 0.9 copy-start.4
  299.3 20.0 %collective-permute-start.6 = (bf16[2,8,192,128]{3,2,1,0:T(8,128)(2,1)}, bf16[2,8,192,128]{3,2,1,0:T(8,128)(2,1)S(1)}, u32[]{:S(2)}, u32[]{:S(2)}) collective-permute-start(bf16[2,8,192,128]{3,2,1,0:T(8,128)(2,1)} %shard_map.120.mine_ref), channel_id=1, source_target_pairs={{0,8},{8,0},{16,24},{24,16},{1,9},{9,1},{17,25},{25,17},{2,10},{10... | collective-permute-start | bytes 2359304 | tf_op jit(solution)/shard_map/ppermute | solution.py:205
  312.3 0.9 copy-start.5
  315.5 7.6 %collective-permute-start.4 = (bf16[2,8,192,128]{3,2,1,0:T(8,128)(2,1)}, bf16[2,8,192,128]{3,2,1,0:T(8,128)(2,1)S(1)}, u32[]{:S(2)}, u32[]{:S(2)}) collective-permute-start(bf16[2,8,192,128]{3,2,1,0:T(8,128)(2,1)} %shard_map.119.mine_ref), channel_id=1, source_target_pairs={{0,8},{8,0},{16,24},{24,16},{1,9},{9,1},{17,25},{25,17},{2,10},{10... | collective-permute-start | bytes 2359304 | tf_op jit(solution)/shard_map/ppermute | solution.py:205
  315.5 0.9 copy-start.3
  319.3 0.9 copy-start.10
  323.1 0.9 copy-start.9
where the time goes:
time: 328 us; the launch traced here: 327 us
  Pallas kernels  262 us (80%)
  waiting for transfers between devices  46.2 us (14%)
  local copies, waits for them, and re-layouts  11.5 us (4%)
  starting transfers between devices  3.83 us (1%)
    pallas_call x1, Pallas kernels, pipeline(): pl.pallas_call(functools.partial(pipeline_body, lanes, far, cuts), in_spe...  215 us
    ppermute x9, waiting for transfers between devices, swap(): return lax.ppermute(value, 'grp', [(g, g ^ bit) for g in range(groups)])  46.2 us
    pallas_call x3, Pallas kernels, last_columns(): pl.pallas_call(functools.partial(last_body, lanes), grid=(inner,), in_spe...  24.4 us
    pallas_call x6, Pallas kernels, blend(): pl.pallas_call(functools.partial(blend_body, count, scales), grid=(group...  13.8 us
    unnamed x24, local copies, waits for them, and re-layouts  10.5 us
    pallas_call x3, Pallas kernels, place_moments(): pl.pallas_call(place_body, grid=(group // 4,), in_specs=[pl.BlockSpec(mem...  8.65 us
  transfers between devices with their start and end apart: 9, of which 6 were waited for; matrix products, arithmetic and copies ran while one was open for 0% of the time, Pallas kernels for 5%

commit v1 on v0

--- a/solution.py
+++ b/solution.py
@@ -206,7 +206,7 @@
 
 
 def join(a, b, count):
-    a, b = a.astype(F32), b.astype(F32)
+    a, b = [v.astype(F32) for v in a], [v.astype(F32) for v in b]
     total = a[0] + b[0]
     spread = (a[1] + b[1]) + jnp.square(a[0] - b[0]) * (0.5 / count)
     return total, spread
@@ -319,16 +319,16 @@
 MESH = pl.DeviceIdType.MESH
 
 
-def pipeline_body(lanes, far, cuts, grid_ref, noise_ref, table_t_ref, turned_ref, diffusion_ref, first_ref, bias_ref,
-                  middle_ref, last_ref, state_ref, table_out, *rest):
+def pipeline_body(lanes, far, cuts, grid_ref, noise_ref, table_t_ref, turned_ref, diffusion_ref, input_ref, extra_ref,
+                  bias_ref, middle_ref, last_ref, state_ref, table_out, first_out, held_out, *rest):
     fields = rest[:lanes]
-    (kept, sent, own, other, back, blocks_ref, basis, flipped, table_ref, damping, rows_in, noise_in,
-     rows_out) = rest[lanes:lanes + 13]
-    rest = rest[lanes + 13:]
+    (kept, sent, own, other, back, blocks_ref, basis, flipped, table_ref, first_ref, damping, rows_in, noise_in,
+     rows_out, held_in, mine, give, taken, held) = rest[lanes:lanes + 19]
+    rest = rest[lanes + 19:]
     scratch = rest[:2 * lanes]
-    (row_sem, noise_sem, out_sem, field_sem, table_sem, basis_send, basis_recv, kept_send, kept_recv, own_send, own_recv, back_send,
+    (row_sem, noise_sem, out_sem, field_sem, table_sem, held_sem, give_sem, basis_send, basis_recv, kept_send, kept_recv, own_send, own_recv, back_send,
      back_recv) = rest[2 * lanes:]
-    members, lat_rows, _, channels = grid_ref.shape
+    members, lat_rows, lon_count, channels = grid_ref.shape
     blocks, share, depth = kept.shape[1:4]
     slots, per, totals, _ = own.shape
     ahead = slots // 2
@@ -474,6 +474,34 @@
         return pltpu.make_async_copy(
             rows_out.at[n % 2], state_ref.at[n // groups, pl.ds(at, GROUP)], out_sem.at[n % 2]
         )
+
+    def greet(**target):
+        pl.semaphore_signal(barrier, inc=1, device_id=target, device_id_type=MESH)
+
+    barrier = pltpu.get_barrier_semaphore()
+    for step in range(1, lanes):
+        greet(lat=place * lanes + (lane + step) % lanes)
+    greet(grp=partner)
+
+    @pl.when(leaf)
+    def _():
+        for step in range(lanes):
+            greet(lat=hub_place * lanes + step)
+
+    @pl.when(hub)
+    def _():
+        greet(lat=opposite)
+        for k in range(lanes, blocks):
+            greet(lat=source_lane(k))
+
+    def all_here():
+        @pl.when(leaf)
+        def _():
+            pl.semaphore_wait(barrier, 2 * lanes)
+
+        @pl.when(hub)
+        def _():
+            pl.semaphore_wait(barrier, 1 + blocks)
 
     def analyse_group(n, carry):
         b = n // groups
@@ -579,11 +607,39 @@
         for k in range(1, blocks):
             back_copy(b, q, k).start()
 
+    def spread_fields(b, at):
+        for dy in range(lanes):
+            for part in range(2):
+                side = slice(part * channels, (part + 1) * channels)
+                value = back[b, dy, :, pl.ds(at, rows), side].astype(F32)
+                space = jnp.zeros((share, pitch - rows, channels), F32)
+                scratch[2 * dy + part][...] = jnp.concatenate([value, space], axis=1).reshape(-1, channels)
+
+    def column_pair(n, i):
+        waves, states = [], []
+        for t in range(2):
+            waves.append(jnp.concatenate([
+                scratch[2 * dy + part][pl.ds(p * GROUP + 2 * i + t, share, stride=pitch), :]
+                for dy in range(lanes) for p in range(2) for part in range(2)
+            ], axis=0).astype(BF16))
+        smoothed = jnp.dot(table_ref[...], jnp.concatenate(waves, axis=1), preferred_element_type=F32)
+        for t in range(2):
+            flat = smoothed[:, t * channels:(t + 1) * channels]
+            joined = jnp.concatenate([flat.astype(BF16), noise_in[n % 2, 2 * i + t]], axis=1)
+            pre = jnp.dot(joined, first_ref[...], preferred_element_type=F32)
+            one = silu(pre + bias_ref[...]).astype(BF16)
+            two = silu(jnp.dot(one, middle_ref[...], preferred_element_type=F32)).astype(BF16)
+            tendency = jnp.dot(two, last_ref[...], preferred_element_type=F32)
+            state = (flat + tendency).astype(BF16)
+            rows_out[n % 2, 2 * i + t] = state
+            states.append(state)
+        return states
+
     def column_group(b, g):
         n = b * groups + g
         at = pl.multiple_of(g * rows, rows)
 
-        @pl.when(n + 1 < (members - 1) * groups)
+        @pl.when(n <= (members - 1) * groups - 1)
         def _():
             load(noise_ref, n + 1).start()
 
@@ -598,12 +654,7 @@
                         def _():
                             back_arrival(b, q, dy).wait_recv()
 
-        for dy in range(lanes):
-            for part in range(2):
-                side = slice(part * channels, (part + 1) * channels)
-                value = back[b, dy, :, pl.ds(at, rows), side].astype(F32)
-                space = jnp.zeros((share, pitch - rows, channels), F32)
-                scratch[2 * dy + part][...] = jnp.concatenate([value, space], axis=1).reshape(-1, channels)
+        spread_fields(b, at)
         load(noise_ref, n).wait()
 
         @pl.when(n >= 2)
@@ -611,21 +662,7 @@
             store(n - 2).wait()
 
         def pair(i, carry):
-            waves = []
-            for t in range(2):
-                waves.append(jnp.concatenate([
-                    scratch[2 * dy + part][pl.ds(p * GROUP + 2 * i + t, share, stride=pitch), :]
-                    for dy in range(lanes) for p in range(2) for part in range(2)
-                ], axis=0).astype(BF16))
-            smoothed = jnp.dot(table_ref[...], jnp.concatenate(waves, axis=1), preferred_element_type=F32)
-            for t in range(2):
-                flat = smoothed[:, t * channels:(t + 1) * channels]
-                joined = jnp.concatenate([flat.astype(BF16), noise_in[n % 2, 2 * i + t]], axis=1)
-                pre = jnp.dot(joined, first_ref[...], preferred_element_type=F32)
-                one = silu(pre + bias_ref[...]).astype(BF16)
-                two = silu(jnp.dot(one, middle_ref[...], preferred_element_type=F32)).astype(BF16)
-                tendency = jnp.dot(two, last_ref[...], preferred_element_type=F32)
-                rows_out[n % 2, 2 * i + t] = (flat + tendency).astype(BF16)
+            column_pair(n, i)
             return carry
 
         lax.fori_loop(0, GROUP // 2, pair, 0)
@@ -633,6 +670,9 @@
 
     def analyse_member(b, first):
         lax.fori_loop(b * groups, (b + 1) * groups, analyse_group, 0)
+        if first:
+            all_here()
+            send_basis(0)
         for q in range(cuts):
             for dy in range(1, lanes):
                 lane_copy(b, q, dy).start()
@@ -659,8 +699,9 @@
     load(grid_ref, 0).start()
     load(noise_ref, 0).start()
     arrange(0)
-    send_basis(0)
     analyse_member(0, True)
+    first_ref[:channels] = input_ref[...]
+    first_ref[channels:] = extra_ref[...]
     table_ref[...] = table_t_ref[...].T
     degree = lax.broadcasted_iota(jnp.int32, (totals, channels), 0)
     for side in range(2):
@@ -669,6 +710,8 @@
         damping[side] = 1.0 / (1.0 + diffusion_ref[...] * (ratio * ratio))
     table_copy = pltpu.make_async_copy(table_ref, table_out, table_sem)
     table_copy.start()
+    first_copy = pltpu.make_async_copy(first_ref, first_out, held_sem.at[members])
+    first_copy.start()
 
     def tick(t, carry):
         @pl.when(hub)
@@ -699,6 +742,14 @@
     lax.fori_loop(0, chunks + ahead, tick, 0)
 
     last = members - 1
+    final_group = last * groups
+    for n in (final_group - 2, final_group - 1):
+        store(n).wait()
+    held_copies = [
+        pltpu.make_async_copy(state_ref.at[b, pl.ds(0, GROUP)], held_in.at[b], held_sem.at[b]) for b in range(last)
+    ]
+    for copy in held_copies:
+        copy.start()
     for q in range(cuts):
         for dy in range(lanes):
             if dy > 0:
@@ -713,8 +764,41 @@
     for dy in range(1, lanes):
         finals[dy].start()
     finals[0].start()
-    for n in ((members - 1) * groups - 2, (members - 1) * groups - 1):
-        store(n).wait()
+    spread_fields(last, 0)
+    load(noise_ref, final_group).wait()
+    for copy in held_copies:
+        copy.wait()
+
+    def moments_pair(i, carry):
+        states = column_pair(final_group, i)
+        for t in range(2):
+            k = 2 * i + t
+            values = [held_in[b, k].astype(F32) for b in range(last)] + [states[t].astype(F32)]
+            total = functools.reduce(jnp.add, values)
+            mean = total * (1.0 / members)
+            spread = functools.reduce(jnp.add, [jnp.square(v - mean) for v in values])
+            half_lon = lon_count // 2
+            for h in range(2):
+                @pl.when(core == h)
+                def _():
+                    for j, value in enumerate((total, spread)):
+                        mine[j, k] = value[h * half_lon:(h + 1) * half_lon].astype(BF16)
+                        give[j, k] = value[(1 - h) * half_lon:(2 - h) * half_lon].astype(BF16)
+        return carry
+
+    lax.fori_loop(0, GROUP // 2, moments_pair, 0)
+    store(final_group).start()
+    exchange = remote(give, taken, give_sem.at[0], give_sem.at[1], grp=partner)
+    exchange.start()
+    exchange.wait_recv()
+    for k in range(GROUP):
+        pair_sums = join(
+            [mine[0, k], mine[1, k]], [taken[0, k], taken[1, k]], members
+        )
+        for j in range(2):
+            held[j, k] = pair_sums[j].astype(BF16)
+    held_copy = pltpu.make_async_copy(held, held_out, held_sem.at[members + 1])
+    held_copy.start()
 
     def drain(b, carry):
         for q in range(cuts):
@@ -750,11 +834,15 @@
         for dy in range(1, lanes):
             basis_copy(q, dy).wait_send()
     table_copy.wait()
+    first_copy.wait()
     for final in finals:
         final.wait()
-
-
-def pipeline(lanes, far, cuts, grid_state, noise, table_t, turned, diffusion, first, bias, middle, output):
+    exchange.wait_send()
+    store(final_group).wait()
+    held_copy.wait()
+
+
+def pipeline(lanes, far, cuts, grid_state, noise, table_t, turned, diffusion, one, two, bias, middle, output):
     members, lat_rows, lon_count, channels = grid_state.shape
     wave_count = turned.shape[0]
     share = wave_count // 2 // lanes
@@ -763,15 +851,18 @@
     count = far * lanes
     per = share // cuts
     slots = 6
+    sums = (2, GROUP, lon_count // 2, channels)
     vmem = pl.BlockSpec(memory_space=pltpu.VMEM)
     dma = pltpu.SemaphoreType.DMA
     return pl.pallas_call(
         functools.partial(pipeline_body, lanes, far, cuts),
-        in_specs=[WAIT, WAIT, vmem, vmem, vmem, vmem, vmem, vmem, vmem],
-        out_specs=[WAIT] * (2 + lanes),
+        in_specs=[WAIT, WAIT, vmem, vmem, vmem, vmem, vmem, vmem, vmem, vmem],
+        out_specs=[WAIT] * (4 + lanes),
         out_shape=[
-            jax.ShapeDtypeStruct((members - 1, *grid_state.shape[1:]), BF16),
+            jax.ShapeDtypeStruct(grid_state.shape, BF16),
             jax.ShapeDtypeStruct((lon_count, table_t.shape[0]), BF16),
+            jax.ShapeDtypeStruct((2 * channels, middle.shape[0]), BF16),
+            jax.ShapeDtypeStruct(sums, BF16),
         ] + [jax.ShapeDtypeStruct((1, share, depth, 2 * channels), BF16)] * lanes,
         scratch_shapes=[
             pltpu.VMEM((members, count, share, depth, 2 * channels), BF16),
@@ -783,13 +874,18 @@
             pltpu.VMEM((2, entries, count * depth, wave_count), BF16),
             pltpu.VMEM((2, entries, wave_count, count * depth), BF16),
             pltpu.VMEM((lon_count, table_t.shape[0]), BF16),
+            pltpu.VMEM((2 * channels, middle.shape[0]), BF16),
             pltpu.VMEM((2, wave_count, channels), F32),
-        ] + [pltpu.VMEM((2, GROUP, lon_count, channels), BF16)] * 3 + [pltpu.VMEM((share * 3 * GROUP, channels), F32)] * (2 * lanes) + [
+        ] + [pltpu.VMEM((2, GROUP, lon_count, channels), BF16)] * 3 + [
+            pltpu.VMEM((members - 1, GROUP, lon_count, channels), BF16)
+        ] + [pltpu.VMEM(sums, BF16)] * 4 + [pltpu.VMEM((share * 3 * GROUP, channels), F32)] * (2 * lanes) + [
             dma((2,)),
             dma((2,)),
             dma((2,)),
             dma((lanes,)),
             dma,
+            dma((members + 2,)),
+            dma((2,)),
             dma((cuts, lanes + 1)),
             dma((cuts, count + 1)),
             dma((members, cuts, 2 * lanes - 1)),
@@ -800,9 +896,9 @@
             dma((members, cuts, lanes)),
         ],
         compiler_params=pltpu.CompilerParams(
-            has_side_effects=True, vmem_limit_bytes=64000 * 1024
+            has_side_effects=True, vmem_limit_bytes=64000 * 1024, collective_id=0
         ),
-    )(grid_state, noise, table_t, turned, diffusion, first, bias, middle, output)
+    )(grid_state, noise, table_t, turned, diffusion, one, two, bias, middle, output)
 
 
 def last_body(lanes, *refs):
@@ -904,6 +1000,28 @@
     )(*operands)
 
 
+def carry_body(state_ref, _, out_ref):
+    out_ref[...] = state_ref[...]
+
+
+def carry_states(states, new_state):
+    members, _, lon_count, channels = states.shape
+    block = pl.BlockSpec((members, GROUP // 2, lon_count, channels), lambda i: (0, i, 0, 0))
+    return pl.pallas_call(
+        carry_body,
+        grid=(2,),
+        in_specs=[block, WAIT],
+        out_specs=block,
+        out_shape=jax.ShapeDtypeStruct(new_state.shape, new_state.dtype),
+        input_output_aliases={1: 0},
+        cost_estimate=pl.CostEstimate(
+            flops=members * GROUP * lon_count * channels,
+            bytes_accessed=4 * members * GROUP * lon_count * channels,
+            transcendentals=0,
+        ),
+    )(states, new_state)
+
+
 def blend_body(count, scales, one_ref, two_ref, out_ref):
     total, spread = join(one_ref[...], two_ref[...], count)
     out_ref[0] = (total * scales[0]).astype(BF16)
@@ -976,21 +1094,20 @@
     lane = lax.axis_index("lat") % lanes
     core = lax.axis_index("grp") % 2
     table_t = slot_table(lon_count, wave_count, share, lane, lanes)
-    first = jnp.concatenate([input_weight, noise_weight], axis=0)
+    turned = legendre.transpose(1, 0, 2)
+    states, table, first, held, *fields = pipeline(
+        lanes, far, cuts, grid_state, noise_field, table_t, turned, diffusion[None], input_weight, noise_weight,
+        input_bias[None], middle_weight, output_weight,
+    )
     params = (first, input_bias[None], middle_weight, output_weight)
-    turned = legendre.transpose(1, 0, 2)
-    states, table, *fields = pipeline(
-        lanes, far, cuts, grid_state, noise_field, table_t, turned, diffusion[None], *params
-    )
     groups = lax.axis_size("grp")
     flag = core[None].astype(jnp.int32)
     new_state, after, placed = None, [], []
     for q in range(parts):
-        new_state, mine, give = last_columns(
-            fields, flag, noise_field, table, *params, states, q, new_state, after
-        )
-        held = blend(mine, swap(give, 1), members, (1.0, 1.0))
-        after = [held]
+        if q > 0:
+            new_state, mine, give = last_columns(fields, flag, noise_field, table, *params, states, q, new_state, after)
+            held = blend(mine, swap(give, 1), members, (1.0, 1.0))
+            after = [held]
         bit, count = 2, 2 * members
         while bit < groups:
             other = swap(held, bit)
@@ -1000,6 +1117,7 @@
             bit, count = 2 * bit, 2 * count
         partner = swap(held, 1)
         placed = place_moments(flag, held, partner, q, lat_rows, placed)
+    new_state = carry_states(states, new_state)
     return (new_state, *placed)
 
 
@@ -1019,7 +1137,7 @@
         lax.axis_size("lat") % (2 * lanes) == 0
         and units % (16 * lanes) == 0
         and lat_rows % GROUP == 0
-        and lat_rows // GROUP < 7
+        and 2 < lat_rows // GROUP < 7
         and members > 1
         and lax.axis_size("grp") > 2
     )

time: 328 us -> 316 us (0.963)
  Pallas kernels: 262 us -> 255 us
    pallas_call x3 -> x2, Pallas kernels: 24.4 us -> 16.3 us  [last_columns(): pl.pallas_call(functools.partial(last_body, lanes), grid=(inner,), in_spe...]
    ppermute x9 -> x8, waiting for transfers between devices: 46.2 us -> 43.3 us  [swap(): return lax.ppermute(value, 'grp', [(g, g ^ bit) for g in range(groups)])]
    pallas_call x6 -> x5, Pallas kernels: 13.8 us -> 11.5 us  [blend(): pl.pallas_call(functools.partial(blend_body, count, scales), grid=(group...]
    unnamed x24 -> x19, local copies, waits for them, and re-layouts: 10.5 us -> 8.68 us
  transfers between devices with their start and end apart: 9 -> 8, of which waited for: 6 -> 5; matrix products, arithmetic and copies ran while one was open for 0% -> 0% of each run, Pallas kernels for 5% -> 6%
where the time goes in v1:
time: 316 us
  Pallas kernels  255 us (81%)
  waiting for transfers between devices  43.3 us (14%)
  local copies, waits for them, and re-layouts  8.85 us (3%)
  starting transfers between devices  5.43 us (2%)
    pallas_call x1, Pallas kernels, pipeline(): pl.pallas_call(functools.partial(pipeline_body, lanes, far, cuts), in_spe...  215 us
    ppermute x8, waiting for transfers between devices, swap(): return lax.ppermute(value, 'grp', [(g, g ^ bit) for g in range(groups)])  43.3 us
    pallas_call x2, Pallas kernels, last_columns(): pl.pallas_call(functools.partial(last_body, lanes), grid=(inner,), in_spe...  16.3 us
    pallas_call x5, Pallas kernels, blend(): pl.pallas_call(functools.partial(blend_body, count, scales), grid=(group...  11.5 us
    unnamed x19, local copies, waits for them, and re-layouts  8.68 us
    pallas_call x3, Pallas kernels, place_moments(): pl.pallas_call(place_body, grid=(group // 4,), in_specs=[pl.BlockSpec(mem...  8.65 us
  transfers between devices with their start and end apart: 8, of which 5 were waited for; matrix products, arithmetic and copies ran while one was open for 0% of the time, Pallas kernels for 6%

profile of v1, /device:TPU:0, one launch (start us, length us, event | category | flops | bytes accessed | tf_op | source)
XLA Modules:
  0.0 315.6 jit_solution(10684101279482220574)
XLA Ops:
  1.0 0.1 mul.60
  1.1 2.5 copy.20
  3.7 2.5 fusion.4.table_t_ref
  6.1 215.0 %shard_map.112 = (bf16[4,24,384,128]{3,2,1,0:T(8,128)(2,1)}, bf16[384,256]{1,0:T(8,128)(2,1)}, bf16[256,256]{1,0:T(8,128)(2,1)}, bf16[2,8,192,128]{3,2,1,0:T(8,1...) custom-call(bf16[4,24,384,128]{3,2,1,0:T(8,128)(2,1)} %grid_ref.1, ...), custom_call_target="tpu_custom_call" | custom-call | tf_op jit(solution)/shard_map/pallas_call | solution.py:857
  221.2 8.1 %shard_map.113 = (bf16[4,24,384,128]{3,2,1,0:T(8,128)(2,1)}, bf16[2,8,192,128]{3,2,1,0:T(8,128)(2,1)}, bf16[2,8,192,128]{3,2,1,0:T(8,128)(2,1)}) custom-call(s32[1]{0:T(128)} %bitcast.3.refs_0_.core_ref, bf16[1,32,48,256]{3,2,1,0:T(8,128)(2,1)} %get-tuple-element.22.refs_1_, bf16[1,32,48,256]{3,2,1,0:T(8,128)(2,1)} %get-tuple-element.23.refs_2_, ...), custom_call_target="tpu_custom_call" | custom-call | flops 1207959552 | bytes 6291456 | tf_op jit(solution)/shard_map/pallas_call | solution.py:983
  229.3 1.5 collective-permute-start
  230.8 2.1 collective-permute-done.two_ref
  232.9 0.9 copy-done.6
  233.8 2.3 shard_map.114.refs_11_.one_ref
  236.1 8.2 %shard_map.115 = (bf16[4,24,384,128]{3,2,1,0:T(8,128)(2,1)}, bf16[2,8,192,128]{3,2,1,0:T(8,128)(2,1)}, bf16[2,8,192,128]{3,2,1,0:T(8,128)(2,1)}) custom-call(s32[1]{0:T(128)} %bitcast.3.refs_0_.core_ref, bf16[1,32,48,256]{3,2,1,0:T(8,128)(2,1)} %get-tuple-element.22.refs_1_, ...), custom_call_target="tpu_custom_call", output_to_operand_aliasing={{0}: (10, {})} | custom-call | flops 1207959552 | bytes 6291456 | tf_op jit(solution)/shard_map/pallas_call | solution.py:983
  244.3 0.4 collective-permute-start.1
  244.7 1.5 collective-permute-start.6
  246.2 0.5 collective-permute-start.4
  246.7 0.1 collective-permute-done.1.two_ref
  246.8 0.9 copy-done.5
  247.7 2.3 shard_map.117.one_ref
  249.9 1.5 collective-permute-start.2
  251.4 13.8 %collective-permute-done.6.two_ref = bf16[2,8,192,128]{3,2,1,0:T(8,128)(2,1)} collective-permute-done((bf16[2,8,192,128]{3,2,1,0:T(8,128)(2,1)S(1)}, bf16[2,8,192,128]{3,2,1,0:T(8,128)(2,1)}, u32[]{:S(2)}, u32[]{:S(2)}) %collective-permute-start.6) | collective-permute-done | bytes 786464 | tf_op jit(solution)/shard_map/ppermute | solution.py:205
  265.2 2.3 shard_map.120.mine_ref
  267.5 14.5 %collective-permute-done.4.two_ref = bf16[2,8,192,128]{3,2,1,0:T(8,128)(2,1)S(1)} collective-permute-done((bf16[2,8,192,128]{3,2,1,0:T(8,128)(2,1)S(1)}, bf16[2,8,192,128]{3,2,1,0:T(8,128)(2,1)S(1)}, u32[]{:S(2)}, u32[]{:S(2)}) %collective-permute-start.4) | collective-permute-done | bytes 786464 | tf_op jit(solution)/shard_map/ppermute | solution.py:205
  281.9 0.9 copy-done.3
  282.8 2.3 shard_map.119.mine_ref
  285.1 12.8 %collective-permute-done.2.two_ref = bf16[2,8,192,128]{3,2,1,0:T(8,128)(2,1)S(1)} collective-permute-done((bf16[2,8,192,128]{3,2,1,0:T(8,128)(2,1)}, bf16[2,8,192,128]{3,2,1,0:T(8,128)(2,1)S(1)}, u32[]{:S(2)}, u32[]{:S(2)}) %collective-permute-start.2) | collective-permute-done | bytes 786464 | tf_op jit(solution)/shard_map/ppermute | solution.py:205
  298.0 0.9 copy-done.4
  298.8 2.3 shard_map.118.mine_ref
  301.1 3.2 %shard_map.116 = bf16[4,24,384,128]{3,2,1,0:T(8,128)(2,1)} custom-call(bf16[4,24,384,128]{3,2,1,0:T(8,128)(2,1)} %get-tuple-element.21.refs_9_.state_ref, bf16[4,24,384,128]{3,2,1,0:T(8,128)(2,1)} %get-tuple-element.29._), custom_call_target="tpu_custom_call", output_to_operand_aliasing={{}: (1, {})} | custom-call | flops 1572864 | bytes 6291456 | tf_op jit(solution)/shard_map/pallas_call | solution.py:1010
  304.3 0.9 copy-done.1
  305.2 2.9 shard_map.121
  308.1 0.9 copy-done.8
  309.0 2.9 shard_map.122
  311.9 0.9 copy-done.7
  312.8 2.9 shard_map.123
  (25 shorter events, 0.4 us)
Async XLA Ops:
  229.3 3.7 %collective-permute-start = (bf16[2,8,192,128]{3,2,1,0:T(8,128)(2,1)}, bf16[2,8,192,128]{3,2,1,0:T(8,128)(2,1)S(1)}, u32[]{:S(2)}, u32[]{:S(2)}) collective-permute-start(bf16[2,8,192,128]{3,2,1,0:T(8,128)(2,1)} %get-tuple-element.28), channel_id=1, source_target_pairs={{0,8},{8,0},{16,24},{24,16},{1,9},{9,1},{17,25},{25,17},{2,10},{10... | collective-permute-start | bytes 2359304 | tf_op jit(solution)/shard_map/ppermute | solution.py:205
  232.9 0.9 copy-start.6
  236.1 8.6 %copy-start.2 = (bf16[2,8,192,128]{3,2,1,0:T(8,128)(2,1)S(1)}, bf16[2,8,192,128]{3,2,1,0:T(8,128)(2,1)}, u32[]{:S(2)}) copy-start(bf16[2,8,192,128]{3,2,1,0:T(8,128)(2,1)} %get-tuple-element.32.one_ref) | copy-start | bytes 2359300
  236.1 10.1 %copy-start = (bf16[2,8,192,128]{3,2,1,0:T(8,128)(2,1)S(1)}, bf16[2,8,192,128]{3,2,1,0:T(8,128)(2,1)}, u32[]{:S(2)}) copy-start(bf16[2,8,192,128]{3,2,1,0:T(8,128)(2,1)} %shard_map.114.refs_11_.one_ref) | copy-start | bytes 2359300
  244.3 2.5 collective-permute-start.1
  244.7 20.5 %collective-permute-start.6 = (bf16[2,8,192,128]{3,2,1,0:T(8,128)(2,1)S(1)}, bf16[2,8,192,128]{3,2,1,0:T(8,128)(2,1)}, u32[]{:S(2)}, u32[]{:S(2)}) collective-permute-start(bf16[2,8,192,128]{3,2,1,0:T(8,128)(2,1)S(1)} %copy-done.2), channel_id=1, source_target_pairs={{0,16},{8,24},{16,0},{24,8},{1,17},{9,25},{17,1},{25,9},{2,18},{10... | collective-permute-start | bytes 2359304 | tf_op jit(solution)/shard_map/ppermute | solution.py:205
  246.2 35.8 %collective-permute-start.4 = (bf16[2,8,192,128]{3,2,1,0:T(8,128)(2,1)S(1)}, bf16[2,8,192,128]{3,2,1,0:T(8,128)(2,1)S(1)}, u32[]{:S(2)}, u32[]{:S(2)}) collective-permute-start(bf16[2,8,192,128]{3,2,1,0:T(8,128)(2,1)S(1)} %copy-done), channel_id=1, source_target_pairs={{0,16},{8,24},{16,0},{24,8},{1,17},{9,25},{17,1},{25,9},{2,18},{10... | collective-permute-start | bytes 2359304 | tf_op jit(solution)/shard_map/ppermute | solution.py:205
  246.8 0.9 copy-start.5
  249.9 48.0 %collective-permute-start.2 = (bf16[2,8,192,128]{3,2,1,0:T(8,128)(2,1)}, bf16[2,8,192,128]{3,2,1,0:T(8,128)(2,1)S(1)}, u32[]{:S(2)}, u32[]{:S(2)}) collective-permute-start(bf16[2,8,192,128]{3,2,1,0:T(8,128)(2,1)} %shard_map.117.one_ref), channel_id=1, source_target_pairs={{0,16},{8,24},{16,0},{24,8},{1,17},{9,25},{17,1},{25,9},{2,18},{10... | collective-permute-start | bytes 2359304 | tf_op jit(solution)/shard_map/ppermute | solution.py:205
  267.5 36.9 %collective-permute-start.7 = (bf16[2,8,192,128]{3,2,1,0:T(8,128)(2,1)}, bf16[2,8,192,128]{3,2,1,0:T(8,128)(2,1)S(1)}, u32[]{:S(2)}, u32[]{:S(2)}) collective-permute-start(bf16[2,8,192,128]{3,2,1,0:T(8,128)(2,1)} %shard_map.120.mine_ref), channel_id=1, source_target_pairs={{0,8},{8,0},{16,24},{24,16},{1,9},{9,1},{17,25},{25,17},{2,10},{10... | collective-permute-start | bytes 2359304 | tf_op jit(solution)/shard_map/ppermute | solution.py:205
  281.9 0.9 copy-start.3
  285.1 23.0 %collective-permute-start.5 = (bf16[2,8,192,128]{3,2,1,0:T(8,128)(2,1)}, bf16[2,8,192,128]{3,2,1,0:T(8,128)(2,1)S(1)}, u32[]{:S(2)}, u32[]{:S(2)}) collective-permute-start(bf16[2,8,192,128]{3,2,1,0:T(8,128)(2,1)} %shard_map.119.mine_ref), channel_id=1, source_target_pairs={{0,8},{8,0},{16,24},{24,16},{1,9},{9,1},{17,25},{25,17},{2,10},{10... | collective-permute-start | bytes 2359304 | tf_op jit(solution)/shard_map/ppermute | solution.py:205
  298.0 0.9 copy-start.4
  301.1 10.7 %collective-permute-start.3 = (bf16[2,8,192,128]{3,2,1,0:T(8,128)(2,1)}, bf16[2,8,192,128]{3,2,1,0:T(8,128)(2,1)S(1)}, u32[]{:S(2)}, u32[]{:S(2)}) collective-permute-start(bf16[2,8,192,128]{3,2,1,0:T(8,128)(2,1)} %shard_map.118.mine_ref), channel_id=1, source_target_pairs={{0,8},{8,0},{16,24},{24,16},{1,9},{9,1},{17,25},{25,17},{2,10},{10... | collective-permute-start | bytes 2359304 | tf_op jit(solution)/shard_map/ppermute | solution.py:205
  304.3 0.9 copy-start.1
  308.1 0.9 copy-start.8
  311.9 0.9 copy-start.7

commit v2 on v1

--- a/solution.py
+++ b/solution.py
@@ -319,20 +319,20 @@
 MESH = pl.DeviceIdType.MESH
 
 
-def pipeline_body(lanes, far, cuts, grid_ref, noise_ref, table_t_ref, turned_ref, diffusion_ref, input_ref, extra_ref,
+def pipeline_body(lanes, far, cuts, grid_ref, noise_ref, table_t_ref, legendre_ref, diffusion_ref, input_ref, extra_ref,
                   bias_ref, middle_ref, last_ref, state_ref, table_out, first_out, held_out, *rest):
     fields = rest[:lanes]
     (kept, sent, own, other, back, blocks_ref, basis, flipped, table_ref, first_ref, damping, rows_in, noise_in,
-     rows_out, held_in, mine, give, taken, held) = rest[lanes:lanes + 19]
-    rest = rest[lanes + 19:]
+     rows_out, held_in, mine, give, taken, held, turned) = rest[lanes:lanes + 20]
+    rest = rest[lanes + 20:]
     scratch = rest[:2 * lanes]
     (row_sem, noise_sem, out_sem, field_sem, table_sem, held_sem, give_sem, basis_send, basis_recv, kept_send, kept_recv, own_send, own_recv, back_send,
-     back_recv) = rest[2 * lanes:]
+     back_recv, piece_send, piece_recv) = rest[2 * lanes:]
     members, lat_rows, lon_count, channels = grid_ref.shape
     blocks, share, depth = kept.shape[1:4]
     slots, per, totals, _ = own.shape
     ahead = slots // 2
-    wave_count = turned_ref.shape[0]
+    wave_count = legendre_ref.shape[1]
     pieces = per // 2
     groups = lat_rows // GROUP
     rows = 2 * GROUP
@@ -394,6 +394,9 @@
         def _():
             basis_own(q).start()
 
+    def waves_of(wave):
+        return turned[pl.ds(pl.multiple_of(wave * lat_rows, GROUP), lat_rows), :]
+
     def arrange(q):
         row = lax.broadcasted_iota(jnp.int32, (lat_rows, totals), 1)
         flip = lax.broadcasted_iota(jnp.int32, (totals, totals), 0)
@@ -406,9 +409,9 @@
                 unit = turn * share + q * per + core * pieces + e
                 if e == pieces:
                     unit = turn * share + wave_count // 2 * (1 - (turn + lanes - 1) // lanes)
-                near = turned_ref[unit].astype(F32)
+                near = waves_of(unit)
                 mirrored = jnp.dot(
-                    turned_ref[(wave_count - unit) % wave_count], flip, preferred_element_type=F32
+                    waves_of((wave_count - unit) % wave_count).astype(BF16), flip, preferred_element_type=F32
                 )
                 near = jnp.where(row >= unit, near, 0.0).reshape(groups, 1, GROUP, totals)
                 mirrored = jnp.where(row < unit, mirrored, 0.0).reshape(groups, 1, GROUP, totals)
@@ -463,6 +466,21 @@
     def back_arrival(b, q, dy):
         part = back.at[b, dy, pl.ds(q * per, per)]
         return remote(part, part, back_send.at[b, q, 0], back_recv.at[b, q, dy], lat=opposite)
+
+    def piece_copy(k, g):
+        b, q = members - 1, cuts - 1
+        units, lats = pl.ds(q * per, per), pl.ds(g * rows, rows)
+        return remote(
+            kept.at[b, k, units, lats], back.at[b, k % lanes, units, lats],
+            back_send.at[b, q, k - 1] if g == 0 else piece_send.at[k - 1, g - 1],
+            back_recv.at[b, q, k % lanes] if g == 0 else piece_recv.at[k % lanes, g - 1], lat=source_lane(k),
+        )
+
+    def piece_arrival(dy, g):
+        b, q = members - 1, cuts - 1
+        part = back.at[b, dy, pl.ds(q * per, per), pl.ds(g * rows, rows)]
+        recv = back_recv.at[b, q, dy] if g == 0 else piece_recv.at[dy, g - 1]
+        return remote(part, part, back_send.at[b, q, 0], recv, lat=opposite)
 
     def load(ref, n):
         at = pl.multiple_of(n % groups * GROUP, GROUP)
@@ -604,8 +622,16 @@
             grid = jnp.dot(basis[0, pieces], damped(0, mark, side), preferred_element_type=F32).astype(BF16)
             put(0, grid, side)
 
-        for k in range(1, blocks):
-            back_copy(b, q, k).start()
+        @pl.when(c < chunks - 1)
+        def _():
+            for k in range(1, blocks):
+                back_copy(b, q, k).start()
+
+        @pl.when(c == chunks - 1)
+        def _():
+            for g in range(groups):
+                for k in range(1, blocks):
+                    piece_copy(k, g).start()
 
     def spread_fields(b, at):
         for dy in range(lanes):
@@ -698,6 +724,8 @@
 
     load(grid_ref, 0).start()
     load(noise_ref, 0).start()
+    for k in range(lat_rows):
+        turned[pl.ds(k, wave_count, stride=lat_rows), :] = legendre_ref[k].astype(F32)
     arrange(0)
     analyse_member(0, True)
     first_ref[:channels] = input_ref[...]
@@ -750,20 +778,59 @@
     ]
     for copy in held_copies:
         copy.start()
+
+    def drain(b, carry):
+        for q in range(cuts):
+            for dy in range(1, lanes):
+                lane_copy(b, q, dy).wait_send()
+
+            @pl.when(leaf)
+            def _():
+                for dy in range(lanes):
+                    kept_copy(b, q, dy).wait_send()
+
+            @pl.when(hub & (b < last) if q == cuts - 1 else hub)
+            def _():
+                for k in range(1, blocks):
+                    back_copy(b, q, k).wait_send()
+        return carry
+
+    lax.fori_loop(0, members, drain, 0)
+
+    @pl.when(hub)
+    def _():
+        for q in range(cuts):
+            basis_swap(q, *span(q)).wait_send()
+        for c in range(chunks - slots, chunks):
+            own_copy(c).wait_send()
+
+    @pl.when(leaf)
+    def _():
+        for q in range(cuts):
+            basis_copy(q, 0).wait_send()
+
     for q in range(cuts):
-        for dy in range(lanes):
-            if dy > 0:
+        for dy in range(1, lanes):
+            basis_copy(q, dy).wait_send()
+
+    def arrived(dy, g):
+        if g == 0:
+            for q in range(cuts - 1):
                 back_arrival(last, q, dy).wait_recv()
-            else:
-                @pl.when(leaf)
-                def _():
-                    back_arrival(last, q, dy).wait_recv()
+        piece_arrival(dy, g).wait_recv()
+
+    def all_arrived(g):
+        for dy in range(1, lanes):
+            arrived(dy, g)
+
+        @pl.when(leaf)
+        def _():
+            arrived(0, g)
+
+    all_arrived(0)
     finals = [
         pltpu.make_async_copy(back.at[last, dy], fields[dy].at[0], field_sem.at[dy]) for dy in range(lanes)
     ]
-    for dy in range(1, lanes):
-        finals[dy].start()
-    finals[0].start()
     spread_fields(last, 0)
     load(noise_ref, final_group).wait()
     for copy in held_copies:
@@ -790,6 +857,10 @@
     store(final_group).start()
     exchange = remote(give, taken, give_sem.at[0], give_sem.at[1], grp=partner)
     exchange.start()
+    for g in range(1, groups):
+        all_arrived(g)
+    for final in finals:
+        final.start()
     exchange.wait_recv()
     for k in range(GROUP):
         pair_sums = join(
@@ -800,39 +871,12 @@
     held_copy = pltpu.make_async_copy(held, held_out, held_sem.at[members + 1])
     held_copy.start()
 
-    def drain(b, carry):
-        for q in range(cuts):
-            for dy in range(1, lanes):
-                lane_copy(b, q, dy).wait_send()
-
-            @pl.when(leaf)
-            def _():
-                for dy in range(lanes):
-                    kept_copy(b, q, dy).wait_send()
-
-            @pl.when(hub)
-            def _():
-                for k in range(1, blocks):
-                    back_copy(b, q, k).wait_send()
-        return carry
-
-    lax.fori_loop(0, members, drain, 0)
-
     @pl.when(hub)
     def _():
-        for q in range(cuts):
-            basis_swap(q, *span(q)).wait_send()
-        for c in range(chunks - slots, chunks):
-            own_copy(c).wait_send()
-
-    @pl.when(leaf)
-    def _():
-        for q in range(cuts):
-            basis_copy(q, 0).wait_send()
-
-    for q in range(cuts):
-        for dy in range(1, lanes):
-            basis_copy(q, dy).wait_send()
+        for g in range(groups):
+            for k in range(1, blocks):
+                piece_copy(k, g).wait_send()
+
     table_copy.wait()
     first_copy.wait()
     for final in finals:
@@ -842,12 +886,13 @@
     held_copy.wait()
 
 
-def pipeline(lanes, far, cuts, grid_state, noise, table_t, turned, diffusion, one, two, bias, middle, output):
+def pipeline(lanes, far, cuts, grid_state, noise, table_t, legendre, diffusion, one, two, bias, middle, output):
     members, lat_rows, lon_count, channels = grid_state.shape
-    wave_count = turned.shape[0]
+    wave_count = legendre.shape[1]
     share = wave_count // 2 // lanes
     entries = share // 2 + 1
     depth = 2 * lat_rows
+    groups = lat_rows // GROUP
     count = far * lanes
     per = share // cuts
     slots = 6
@@ -878,7 +923,7 @@
             pltpu.VMEM((2, wave_count, channels), F32),
         ] + [pltpu.VMEM((2, GROUP, lon_count, channels), BF16)] * 3 + [
             pltpu.VMEM((members - 1, GROUP, lon_count, channels), BF16)
-        ] + [pltpu.VMEM(sums, BF16)] * 4 + [pltpu.VMEM((share * 3 * GROUP, channels), F32)] * (2 * lanes) + [
+        ] + [pltpu.VMEM(sums, BF16)] * 4 + [pltpu.VMEM((wave_count * lat_rows, wave_count), F32)] + [pltpu.VMEM((share * 3 * GROUP, channels), F32)] * (2 * lanes) + [
             dma((2,)),
             dma((2,)),
             dma((2,)),
@@ -894,11 +939,13 @@
             dma((members * cuts,)),
             dma((members, cuts, count - 1)),
             dma((members, cuts, lanes)),
+            dma((count - 1, groups - 1)),
+            dma((lanes, groups - 1)),
         ],
         compiler_params=pltpu.CompilerParams(
             has_side_effects=True, vmem_limit_bytes=64000 * 1024, collective_id=0
         ),
-    )(grid_state, noise, table_t, turned, diffusion, one, two, bias, middle, output)
+    )(grid_state, noise, table_t, legendre, diffusion, one, two, bias, middle, output)
 
 
 def last_body(lanes, *refs):
@@ -1037,40 +1084,45 @@
         in_specs=[block, block],
         out_specs=block,
         out_shape=jax.ShapeDtypeStruct(one.shape, BF16),
+        compiler_params=pltpu.CompilerParams(vmem_limit_bytes=64000 * 1024),
         cost_estimate=pl.CostEstimate(
             flops=4 * one.size, bytes_accessed=6 * one.size, transcendentals=0
         ),
     )(one, two)
 
 
-def place_body(core_ref, mine_ref, partner_ref, *refs):
+def place_body(count, core_ref, mine_ref, other_ref, beside_ref, crossed_ref, *refs):
     outs = refs[-2:]
     half = mine_ref.shape[2]
+    scales = (0.5 / count, 1.0 / (2 * count - 1))
+    own = join(mine_ref[...], other_ref[...], count)
+    partner = join(beside_ref[...], crossed_ref[...], count)
     for h in range(2):
         @pl.when(core_ref[0] == h)
         def _():
             for j in range(2):
-                outs[j][:, h * half:(h + 1) * half] = mine_ref[j].astype(F32)
-                outs[j][:, (1 - h) * half:(2 - h) * half] = partner_ref[j].astype(F32)
-
-
-def place_moments(core, mine, partner, part, lat_rows, previous):
-    _, group, half, channels = mine.shape
+                outs[j][:, h * half:(h + 1) * half] = own[j] * scales[j]
+                outs[j][:, (1 - h) * half:(2 - h) * half] = partner[j] * scales[j]
+
+
+def place_moments(core, sums, count, part, lat_rows, previous):
+    _, group, half, channels = sums[0].shape
     shape = (lat_rows, 2 * half, channels)
     block = pl.BlockSpec((2, 4, half, channels), lambda i: (0, i, 0, 0))
     return pl.pallas_call(
-        place_body,
+        functools.partial(place_body, count),
         grid=(group // 4,),
-        in_specs=[pl.BlockSpec(memory_space=pltpu.SMEM), block, block] + [WAIT] * len(previous),
+        in_specs=[pl.BlockSpec(memory_space=pltpu.SMEM)] + [block] * 4 + [WAIT] * len(previous),
         out_specs=[
             pl.BlockSpec((4, 2 * half, channels), lambda i: (part * (group // 4) + i, 0, 0))
         ] * 2,
         out_shape=[jax.ShapeDtypeStruct(shape, F32)] * 2,
-        input_output_aliases={3 + j: j for j in range(len(previous))},
+        input_output_aliases={5 + j: j for j in range(len(previous))},
+        compiler_params=pltpu.CompilerParams(vmem_limit_bytes=64000 * 1024),
         cost_estimate=pl.CostEstimate(
-            flops=4 * mine.size, bytes_accessed=16 * mine.size, transcendentals=0
+            flops=16 * sums[0].size, bytes_accessed=24 * sums[0].size, transcendentals=0
         ),
-    )(core, mine, partner, *previous)
+    )(core, *sums, *previous)
 
 
 def hub_plan(
@@ -1094,9 +1146,8 @@
     lane = lax.axis_index("lat") % lanes
     core = lax.axis_index("grp") % 2
     table_t = slot_table(lon_count, wave_count, share, lane, lanes)
-    turned = legendre.transpose(1, 0, 2)
     states, table, first, held, *fields = pipeline(
-        lanes, far, cuts, grid_state, noise_field, table_t, turned, diffusion[None], input_weight, noise_weight,
+        lanes, far, cuts, grid_state, noise_field, table_t, legendre, diffusion[None], input_weight, noise_weight,
         input_bias[None], middle_weight, output_weight,
     )
     params = (first, input_bias[None], middle_weight, output_weight)
@@ -1106,17 +1157,17 @@
     for q in range(parts):
         if q > 0:
             new_state, mine, give = last_columns(fields, flag, noise_field, table, *params, states, q, new_state, after)
-            held = blend(mine, swap(give, 1), members, (1.0, 1.0))
+            given = swap(give, 1)
+            held = blend(mine, given, members, (1.0, 1.0))
             after = [held]
         bit, count = 2, 2 * members
-        while bit < groups:
-            other = swap(held, bit)
-            final = 2 * bit >= groups
-            scales = (0.5 / count, 1.0 / (2 * count - 1)) if final else (1.0, 1.0)
-            held = blend(held, other, count, scales)
+        while 2 * bit < groups:
+            held = blend(held, swap(held, bit), count, (1.0, 1.0))
             bit, count = 2 * bit, 2 * count
-        partner = swap(held, 1)
-        placed = place_moments(flag, held, partner, q, lat_rows, placed)
+        beside = swap(held, 1)
+        other = swap(held, bit)
+        crossed = swap(other, 1)
+        placed = place_moments(flag, (held, other, beside, crossed), count, q, lat_rows, placed)
     new_state = carry_states(states, new_state)
     return (new_state, *placed)
 

time: 316 us -> 310 us (0.981)
  local copies, waits for them, and re-layouts: 8.85 us -> 1.05 us
  waiting for transfers between devices: 43.3 us -> 48.9 us
  Pallas kernels: 255 us -> 250 us
    unnamed x19 -> x4, local copies, waits for them, and re-layouts: 8.68 us -> 0.88 us
    pallas_call x5 -> x2, Pallas kernels: 11.5 us -> 4.54 us  [blend(): pl.pallas_call(functools.partial(blend_body, count, scales), grid=(group...]
    ppermute x8 -> x11, waiting for transfers between devices: 43.3 us -> 48.9 us  [swap(): return lax.ppermute(value, 'grp', [(g, g ^ bit) for g in range(groups)])]
    ppermute x8 -> x11, starting transfers between devices: 5.43 us -> 6.51 us  [swap(): return lax.ppermute(value, 'grp', [(g, g ^ bit) for g in range(groups)])]
  transfers between devices with their start and end apart: 8 -> 11, of which waited for: 5 -> 5; matrix products, arithmetic and copies ran while one was open for 0% -> 0% of each run, Pallas kernels for 6% -> 4%
where the time goes in v2:
time: 310 us; the launch traced here: 309 us
  Pallas kernels  250 us (81%)
  waiting for transfers between devices  48.9 us (16%)
  starting transfers between devices  6.51 us (2%)
    pallas_call x1, Pallas kernels, pipeline(): pl.pallas_call(functools.partial(pipeline_body, lanes, far, cuts), in_spe...  214 us
    ppermute x11, waiting for transfers between devices, swap(): return lax.ppermute(value, 'grp', [(g, g ^ bit) for g in range(groups)])  48.9 us
    pallas_call x2, Pallas kernels, last_columns(): pl.pallas_call(functools.partial(last_body, lanes), grid=(inner,), in_spe...  16.2 us
    pallas_call x3, Pallas kernels, place_moments(): pl.pallas_call(functools.partial(place_body, count), grid=(group // 4,),...  11.5 us
    ppermute x11, starting transfers between devices, swap(): return lax.ppermute(value, 'grp', [(g, g ^ bit) for g in range(groups)])  6.51 us
  transfers between devices with their start and end apart: 11, of which 5 were waited for; matrix products, arithmetic and copies ran while one was open for 0% of the time, Pallas kernels for 4%

profile of v2, /device:TPU:0, one launch (start us, length us, event | category | flops | bytes accessed | tf_op | source)
XLA Modules:
  0.0 309.5 jit_solution(9204533381902244359)
XLA Ops:
  0.7 0.1 fusion.9
  0.8 0.1 iota_add_fusion
  0.8 0.1 broadcast_select_fusion.1
  0.9 0.1 broadcast_select_fusion
  1.0 0.1 mul.60
  1.1 0.1 select_n.71
  1.1 2.5 fusion.4.table_t_ref
  3.6 214.1 %shard_map.112 = (bf16[4,24,384,128]{3,2,1,0:T(8,128)(2,1)}, bf16[384,256]{1,0:T(8,128)(2,1)}, bf16[256,256]{1,0:T(8,128)(2,1)}, bf16[2,8,192,128]{3,2,1,0:T(8,1...) custom-call(bf16[4,24,384,128]{3,2,1,0:T(8,128)(2,1)} %grid_ref.1, ...), custom_call_target="tpu_custom_call" | custom-call | tf_op jit(solution)/shard_map/pallas_call | solution.py:902
  217.7 8.1 %shard_map.113 = (bf16[4,24,384,128]{3,2,1,0:T(8,128)(2,1)}, bf16[2,8,192,128]{3,2,1,0:T(8,128)(2,1)}, bf16[2,8,192,128]{3,2,1,0:T(8,128)(2,1)}) custom-call(s32[1]{0:T(128)} %bitcast.2.refs_0_.core_ref, bf16[1,32,48,256]{3,2,1,0:T(8,128)(2,1)} %get-tuple-element.22.refs_1_, bf16[1,32,48,256]{3,2,1,0:T(8,128)(2,1)} %get-tuple-element.23.refs_2_, ...), custom_call_target="tpu_custom_call" | custom-call | flops 1207959552 | bytes 6291456 | tf_op jit(solution)/shard_map/pallas_call | solution.py:1030
  225.8 1.5 collective-permute-start
  227.4 2.1 collective-permute-done.two_ref
  229.5 0.9 copy-done.1
  230.4 2.3 shard_map.114.refs_11_.mine_ref
  232.7 8.1 %shard_map.115 = (bf16[4,24,384,128]{3,2,1,0:T(8,128)(2,1)}, bf16[2,8,192,128]{3,2,1,0:T(8,128)(2,1)}, bf16[2,8,192,128]{3,2,1,0:T(8,128)(2,1)}) custom-call(s32[1]{0:T(128)} %bitcast.2.refs_0_.core_ref, bf16[1,32,48,256]{3,2,1,0:T(8,128)(2,1)} %get-tuple-element.22.refs_1_, ...), custom_call_target="tpu_custom_call", output_to_operand_aliasing={{0}: (10, {})} | custom-call | flops 1207959552 | bytes 6291456 | tf_op jit(solution)/shard_map/pallas_call | solution.py:1030
  240.8 0.4 collective-permute-start.1
  241.2 1.5 collective-permute-start.8
  242.7 0.5 collective-permute-start.5
  243.2 0.2 collective-permute-done.1.two_ref
  243.4 2.3 shard_map.117.mine_ref
  245.7 1.5 collective-permute-start.2
  247.2 14.7 %collective-permute-done.8.other_ref = bf16[2,8,192,128]{3,2,1,0:T(8,128)(2,1)} collective-permute-done((bf16[2,8,192,128]{3,2,1,0:T(8,128)(2,1)}, bf16[2,8,192,128]{3,2,1,0:T(8,128)(2,1)}, u32[]{:S(2)}, u32[]{:S(2)}) %collective-permute-start.8) | collective-permute-done | bytes 786464 | tf_op jit(solution)/shard_map/ppermute | solution.py:205
  261.9 0.5 collective-permute-start.6
  262.4 16.3 %collective-permute-done.5.other_ref = bf16[2,8,192,128]{3,2,1,0:T(8,128)(2,1)} collective-permute-done((bf16[2,8,192,128]{3,2,1,0:T(8,128)(2,1)S(1)}, bf16[2,8,192,128]{3,2,1,0:T(8,128)(2,1)}, u32[]{:S(2)}, u32[]{:S(2)}) %collective-permute-start.5) | collective-permute-done | bytes 786464 | tf_op jit(solution)/shard_map/ppermute | solution.py:205
  278.8 0.5 collective-permute-start.3
  279.3 15.5 %collective-permute-done.2.other_ref = bf16[2,8,192,128]{3,2,1,0:T(8,128)(2,1)} collective-permute-done((bf16[2,8,192,128]{3,2,1,0:T(8,128)(2,1)}, bf16[2,8,192,128]{3,2,1,0:T(8,128)(2,1)}, u32[]{:S(2)}, u32[]{:S(2)}) %collective-permute-start.2) | collective-permute-done | bytes 786464 | tf_op jit(solution)/shard_map/ppermute | solution.py:205
  294.8 3.2 %shard_map.116 = bf16[4,24,384,128]{3,2,1,0:T(8,128)(2,1)} custom-call(bf16[4,24,384,128]{3,2,1,0:T(8,128)(2,1)} %get-tuple-element.21.refs_9_.state_ref, bf16[4,24,384,128]{3,2,1,0:T(8,128)(2,1)} %get-tuple-element.29._), custom_call_target="tpu_custom_call", output_to_operand_aliasing={{}: (1, {})} | custom-call | flops 1572864 | bytes 6291456 | tf_op jit(solution)/shard_map/pallas_call | solution.py:1057
  297.9 0.0 collective-permute-done.10.crossed_ref
  298.0 3.8 %shard_map.118 = (f32[24,384,128]{2,1,0:T(8,128)}, f32[24,384,128]{2,1,0:T(8,128)}) custom-call(s32[1]{0:T(128)} %bitcast.2.refs_0_.core_ref, bf16[2,8,192,128]{3,2,1,0:T(8,128)(2,1)} %get-tuple-element.32.mine_ref, bf16[2,8,192,128]{3,2,1,0:T(8,128)(2,1)} %collective-permute-done.8.other_ref, bf16[2,8,192,128]{3,2,1,0:T(8,128)(2,1)} %collective-permute-done.9.beside_ref, ...), custom_call_target="tpu_custom_call" | custom-call | flops 6291456 | bytes 9437184 | tf_op jit(solution)/shard_map/pallas_call | solution.py:1112
  301.8 0.0 collective-permute-done.6.beside_ref
  301.8 3.8 %shard_map.119 = (f32[24,384,128]{2,1,0:T(8,128)}, f32[24,384,128]{2,1,0:T(8,128)}) custom-call(s32[1]{0:T(128)} %bitcast.2.refs_0_.core_ref, bf16[2,8,192,128]{3,2,1,0:T(8,128)(2,1)} %shard_map.114.refs_11_.mine_ref, bf16[2,8,192,128]{3,2,1,0:T(8,128)(2,1)} %collective-permute-done.5.other_ref, ...), custom_call_target="tpu_custom_call", output_to_operand_aliasing={{0}: (5, {}), {1}: (6, {})} | custom-call | flops 6291456 | bytes 9437184 | tf_op jit(solution)/shard_map/pallas_call | solution.py:1112
  305.6 0.0 collective-permute-done.3.beside_ref
  305.6 3.8 %shard_map.120 = (f32[24,384,128]{2,1,0:T(8,128)}, f32[24,384,128]{2,1,0:T(8,128)}) custom-call(s32[1]{0:T(128)} %bitcast.2.refs_0_.core_ref, bf16[2,8,192,128]{3,2,1,0:T(8,128)(2,1)} %shard_map.117.mine_ref, bf16[2,8,192,128]{3,2,1,0:T(8,128)(2,1)} %collective-permute-done.2.other_ref, ...), custom_call_target="tpu_custom_call", output_to_operand_aliasing={{0}: (5, {}), {1}: (6, {})} | custom-call | flops 6291456 | bytes 9437184 | tf_op jit(solution)/shard_map/pallas_call | solution.py:1112
  (13 shorter events, 0.0 us)
Async XLA Ops:
  225.8 3.7 %collective-permute-start = (bf16[2,8,192,128]{3,2,1,0:T(8,128)(2,1)}, bf16[2,8,192,128]{3,2,1,0:T(8,128)(2,1)S(1)}, u32[]{:S(2)}, u32[]{:S(2)}) collective-permute-start(bf16[2,8,192,128]{3,2,1,0:T(8,128)(2,1)} %get-tuple-element.28), channel_id=1, source_target_pairs={{0,8},{8,0},{16,24},{24,16},{1,9},{9,1},{17,25},{25,17},{2,10},{10... | collective-permute-start | bytes 2359304 | tf_op jit(solution)/shard_map/ppermute | solution.py:205
  229.5 0.9 copy-start.1
  232.7 10.1 %copy-start = (bf16[2,8,192,128]{3,2,1,0:T(8,128)(2,1)S(1)}, bf16[2,8,192,128]{3,2,1,0:T(8,128)(2,1)}, u32[]{:S(2)}) copy-start(bf16[2,8,192,128]{3,2,1,0:T(8,128)(2,1)} %shard_map.114.refs_11_.mine_ref) | copy-start | bytes 2359300
  240.8 2.6 collective-permute-start.1
  241.2 20.7 %collective-permute-start.8 = (bf16[2,8,192,128]{3,2,1,0:T(8,128)(2,1)}, bf16[2,8,192,128]{3,2,1,0:T(8,128)(2,1)}, u32[]{:S(2)}, u32[]{:S(2)}) collective-permute-start(bf16[2,8,192,128]{3,2,1,0:T(8,128)(2,1)} %get-tuple-element.32.mine_ref), channel_id=1, source_target_pairs={{0,16},{8,24},{16,0},{24,8},{1,17},{9,25},{17,1},{25,9},{2,18},{10... | collective-permute-start | bytes 2359304 | tf_op jit(solution)/shard_map/ppermute | solution.py:205
  242.7 36.0 %collective-permute-start.5 = (bf16[2,8,192,128]{3,2,1,0:T(8,128)(2,1)S(1)}, bf16[2,8,192,128]{3,2,1,0:T(8,128)(2,1)}, u32[]{:S(2)}, u32[]{:S(2)}) collective-permute-start(bf16[2,8,192,128]{3,2,1,0:T(8,128)(2,1)S(1)} %copy-done), channel_id=1, source_target_pairs={{0,16},{8,24},{16,0},{24,8},{1,17},{9,25},{17,1},{25,9},{2,18},{10... | collective-permute-start | bytes 2359304 | tf_op jit(solution)/shard_map/ppermute | solution.py:205
  243.2 35.6 %collective-permute-start.9 = (bf16[2,8,192,128]{3,2,1,0:T(8,128)(2,1)}, bf16[2,8,192,128]{3,2,1,0:T(8,128)(2,1)}, u32[]{:S(2)}, u32[]{:S(2)}) collective-permute-start(bf16[2,8,192,128]{3,2,1,0:T(8,128)(2,1)} %get-tuple-element.32.mine_ref), channel_id=1, source_target_pairs={{0,8},{8,0},{16,24},{24,16},{1,9},{9,1},{17,25},{25,17},{2,10},{10... | collective-permute-start | bytes 2359304 | tf_op jit(solution)/shard_map/ppermute | solution.py:205
  245.7 49.1 %collective-permute-start.2 = (bf16[2,8,192,128]{3,2,1,0:T(8,128)(2,1)}, bf16[2,8,192,128]{3,2,1,0:T(8,128)(2,1)}, u32[]{:S(2)}, u32[]{:S(2)}) collective-permute-start(bf16[2,8,192,128]{3,2,1,0:T(8,128)(2,1)} %shard_map.117.mine_ref), channel_id=1, source_target_pairs={{0,16},{8,24},{16,0},{24,8},{1,17},{9,25},{17,1},{25,9},{2,18},{10... | collective-permute-start | bytes 2359304 | tf_op jit(solution)/shard_map/ppermute | solution.py:205
  261.9 36.0 %collective-permute-start.10 = (bf16[2,8,192,128]{3,2,1,0:T(8,128)(2,1)}, bf16[2,8,192,128]{3,2,1,0:T(8,128)(2,1)}, u32[]{:S(2)}, u32[]{:S(2)}) collective-permute-start(bf16[2,8,192,128]{3,2,1,0:T(8,128)(2,1)} %collective-permute-done.8.other_ref), channel_id=1, source_target_pairs={{0,8},{8,0},{16,24},{24,16},{1,9},{9,1},{17,25},{25,17},{2,10},{10... | collective-permute-start | bytes 2359304 | tf_op jit(solution)/shard_map/ppermute | solution.py:205
  261.9 39.9 %collective-permute-start.6 = (bf16[2,8,192,128]{3,2,1,0:T(8,128)(2,1)S(1)}, bf16[2,8,192,128]{3,2,1,0:T(8,128)(2,1)}, u32[]{:S(2)}, u32[]{:S(2)}) collective-permute-start(bf16[2,8,192,128]{3,2,1,0:T(8,128)(2,1)S(1)} %copy-done), channel_id=1, source_target_pairs={{0,8},{8,0},{16,24},{24,16},{1,9},{9,1},{17,25},{25,17},{2,10},{10... | collective-permute-start | bytes 2359304 | tf_op jit(solution)/shard_map/ppermute | solution.py:205
  278.8 23.0 %collective-permute-start.7 = (bf16[2,8,192,128]{3,2,1,0:T(8,128)(2,1)}, bf16[2,8,192,128]{3,2,1,0:T(8,128)(2,1)}, u32[]{:S(2)}, u32[]{:S(2)}) collective-permute-start(bf16[2,8,192,128]{3,2,1,0:T(8,128)(2,1)} %collective-permute-done.5.other_ref), channel_id=1, source_target_pairs={{0,8},{8,0},{16,24},{24,16},{1,9},{9,1},{17,25},{25,17},{2,10},{10... | collective-permute-start | bytes 2359304 | tf_op jit(solution)/shard_map/ppermute | solution.py:205
  278.8 26.9 %collective-permute-start.3 = (bf16[2,8,192,128]{3,2,1,0:T(8,128)(2,1)}, bf16[2,8,192,128]{3,2,1,0:T(8,128)(2,1)}, u32[]{:S(2)}, u32[]{:S(2)}) collective-permute-start(bf16[2,8,192,128]{3,2,1,0:T(8,128)(2,1)} %shard_map.117.mine_ref), channel_id=1, source_target_pairs={{0,8},{8,0},{16,24},{24,16},{1,9},{9,1},{17,25},{25,17},{2,10},{10... | collective-permute-start | bytes 2359304 | tf_op jit(solution)/shard_map/ppermute | solution.py:205
  294.8 10.9 %collective-permute-start.4 = (bf16[2,8,192,128]{3,2,1,0:T(8,128)(2,1)}, bf16[2,8,192,128]{3,2,1,0:T(8,128)(2,1)}, u32[]{:S(2)}, u32[]{:S(2)}) collective-permute-start(bf16[2,8,192,128]{3,2,1,0:T(8,128)(2,1)} %collective-permute-done.2.other_ref), channel_id=1, source_target_pairs={{0,8},{8,0},{16,24},{24,16},{1,9},{9,1},{17,25},{25,17},{2,10},{10... | collective-permute-start | bytes 2359304 | tf_op jit(solution)/shard_map/ppermute | solution.py:205
